TPU v7x, 512 devices: a whole 4x8x8 slice. The times are simulated.
512 devices in a mesh: sub: 128 (over z, y, core), grp: 4 (over x).
Axes of the slice: x: 4, y: 8, z: 8, core: 2. Of those that a mesh axis runs over, the one named last changes fastest.
Arguments:
- schur: bfloat16 [128, 2048, 2048], P('sub', 'grp'), may hold values from -0.125 to 0.125
- rhs: float32 [128, 2048, 192], P('sub', 'grp'), may hold values from -6 to 6
- start: float32 [128, 2048, 192], P('sub', 'grp'), may hold values from -6 to 6
- project: bfloat16 [128, 32, 4096], P('sub', 'grp'), may hold values from -0.75 to 0.75
- coarse_basis: bfloat16 [128, 8, 2048], P('sub', None, 'grp'), may hold values from -0.375 to 0.375
- owner_of_face: int32 [128, 32, 1], replicated, may hold values from 0 to 4; in each aligned block of 32 rows (0 to 31, 32 to 63, ..., all dimensions but the last counted through in order) at most 8 rows name the same one
- mortar_of_face: int32 [128, 32], replicated, may hold values from 0 to 15
- mortar_order: int32 [128, 16], replicated, may hold values from 3 to 7
- subdomain_map: int32 [128], replicated, may hold values from 0 to 127, each once
- vertex_ids: int32 [128, 8], replicated, may hold values from 0 to 255, all different within a row
Outputs:
- solution: float32 [128, 2048, 192], P('sub', 'grp')
Inputs may be any that keep to these rules, and one draw needn't show every extreme that they name: `owner_of_face`: the 32 faces of one subdomain name one offset at most 8 times. `mortar_of_face`: faces with the same owner and the same number lie on one mortar. `mortar_order`: row o holds the orders of the mortars owned by index o. `subdomain_map`: each subdomain once. `vertex_ids`: the 8 vertices of a subdomain differ; every vertex belongs to some subdomain.
All inputs are finite; a program needn't handle non-finite values.
Results may differ from a plain program's by a relative error of at most 0.0031.
Values may be sent and summed in bfloat16 or wider, within the bound.
A program may use at most 64 MiB of HBM per device.

v0:
```python
import jax
import jax.numpy as jnp
from jax import lax
from jax.sharding import Mesh
from jax.sharding import PartitionSpec as P

DEG = 8
FPTS = 64
MODES = 64
MORT_OWN = 16
ITERS = 2
REACH = 2
CAP = 8
SUB = ("sub_0", "sub_1", "sub_2")


relax_weight = 0.5
coarse_weight = 0.5


def joined_along(parts, dim):
    parts = jnp.moveaxis(parts, 0, dim)
    lengths = parts.shape
    return parts.reshape(*lengths[:dim], lengths[dim] * lengths[dim + 1], *lengths[dim + 2 :])


def sent_to_all(value, axis):
    copies = jnp.broadcast_to(value, (lax.axis_size(axis), *value.shape))
    return lax.all_to_all(copies, axis, split_axis=0, concat_axis=0, tiled=True)


def gathered_copies(value, axis, dim):
    return joined_along(sent_to_all(value, axis), dim)


def passed_along(value, axis, steps):
    count = lax.axis_size(axis)
    pairs = [(source, (source + steps) % count) for source in range(count)]
    return lax.ppermute(value, axis, pairs)


def taken_together(value, axis):
    return sent_to_all(value, axis).sum(axis=0)


def filled_up(lines, length):
    spare = -len(lines) % length
    return jnp.pad(lines, [(0, spare)] + [(0, 0)] * (lines.ndim - 1))


def whole_of(value, axes, dim):
    far, near = axes
    parts = sent_to_all(sent_to_all(value, far), near)
    return joined_along(parts.swapaxes(0, 1).reshape(-1, *value.shape), dim)


def split_up(value, dim, length):
    before, after = (value.shape[:dim], value.shape[dim + 1 :])
    return jnp.moveaxis(value.reshape(*before, length, -1, *after), dim, 0)


def sent_and_summed(value, axis, dim):
    parts = split_up(value, dim, lax.axis_size(axis))
    arrived = lax.all_to_all(parts, axis, split_axis=0, concat_axis=0, tiled=True)
    return arrived.sum(axis=0)


def summed_rows(value, axes, dim):
    far, near = axes
    parts = split_up(value, dim, lax.axis_size(far))
    nearer = sent_and_summed(parts, near, dim + 1)
    arrived = lax.all_to_all(nearer, far, split_axis=0, concat_axis=0, tiled=True)
    return arrived.sum(axis=0)


def sum_by_parts(value, axes):
    lines = value.reshape(-1, value.shape[-1])
    padded = filled_up(lines, lax.axis_size(axes[0]) * lax.axis_size(axes[1]))
    whole = whole_of(summed_rows(padded, axes, 0), axes, 0)
    return lax.slice_in_dim(whole, 0, len(lines)).reshape(value.shape)


def body(
    schur,
    rhs,
    start,
    project,
    coarse_basis,
    owner_of_face,
    mortar_of_face,
    mortar_order,
    subdomain_map,
    vertex_ids,
):
    highest = lax.Precision.HIGHEST
    contract_first = (((0,), (0,)), ((), ()))
    sub_count = lax.axis_size(SUB)
    position = lax.axis_index(SUB)
    all_faces = owner_of_face.shape[1]
    own_faces = project.shape[1]
    own_rows = schur.shape[1]
    neighbours = 2 * REACH + 1
    capacity = CAP
    vertices = 2 * sub_count
    held = jnp.take(owner_of_face[:, :, 0], subdomain_map, axis=0)
    mortar_local = jnp.take(mortar_of_face, subdomain_map, axis=0)
    face_index = jnp.arange(all_faces, dtype=jnp.int32)
    earlier = face_index[None, :] < face_index[:, None]
    ranks = jnp.sum(
        ((held[:, :, None] == held[:, None, :]) & earlier[None, :, :]).astype(jnp.int32), axis=2
    )
    my_held = lax.dynamic_index_in_dim(held, position, 0, keepdims=False)
    my_ranks = lax.dynamic_index_in_dim(ranks, position, 0, keepdims=False)
    slot_ids = my_held * capacity + my_ranks
    send_table = (
        jnp.arange(neighbours * capacity, dtype=jnp.int32)[:, None] == slot_ids[None, :]
    ).astype(jnp.bfloat16)
    links = jnp.arange(neighbours, dtype=jnp.int32)
    senders = jnp.mod(position - links + REACH, sub_count)
    from_held = jnp.take(held, senders, axis=0)
    from_mortar = jnp.take(mortar_local, senders, axis=0)
    from_ranks = jnp.take(ranks, senders, axis=0)
    incoming = (from_held == links[:, None]).astype(jnp.float32)
    mortar_hot = (
        from_mortar[:, :, None] == jnp.arange(MORT_OWN, dtype=jnp.int32)[None, None, :]
    ).astype(jnp.float32)
    rank_hot = (
        from_ranks[:, :, None] == jnp.arange(capacity, dtype=jnp.int32)[None, None, :]
    ).astype(jnp.float32)
    counts = jnp.einsum("jfk,jf->k", mortar_hot, incoming)
    degree = jnp.arange(MODES, dtype=jnp.int32)
    orders = lax.dynamic_index_in_dim(mortar_order, position, 0, keepdims=False)[:, None]
    keep_mask = ((degree[None, :] // DEG <= orders) & (degree[None, :] % DEG <= orders)).astype(
        jnp.float32
    )
    divisor = jnp.maximum(counts, 1.0)
    joined = jnp.einsum("jfk,jfc->kjc", mortar_hot * incoming[:, :, None], rank_hot)
    owner_table = joined.reshape(MORT_OWN, neighbours * capacity).astype(jnp.bfloat16)
    my_corners = lax.dynamic_index_in_dim(
        jnp.take(vertex_ids, subdomain_map, axis=0), position, 0, keepdims=False
    )
    corner_hot = (my_corners[:, None] == jnp.arange(vertices, dtype=jnp.int32)[None, :]).astype(
        jnp.float32
    )
    coarse_wide = coarse_basis[0].astype(jnp.float32)
    tables = project[0].reshape(own_faces, MODES, FPTS)
    matrix = schur[0]
    target = rhs[0]
    traces = start[0]
    for repeat in range(ITERS):
        trace_b = traces.astype(jnp.bfloat16)
        product = jnp.dot(
            matrix, gathered_copies(trace_b, "grp", 0), preferred_element_type=jnp.float32
        )
        residual = (product - target).astype(jnp.bfloat16)
        face_res = residual.reshape(own_faces, FPTS, -1)
        coeffs = jnp.einsum(
            "fmp,fpr->fmr", tables, face_res, preferred_element_type=jnp.float32
        ).astype(jnp.bfloat16)
        grouped = lax.all_to_all(coeffs, "grp", split_axis=2, concat_axis=0, tiled=True)
        part_rhs = grouped.shape[2]
        payload = grouped.reshape(all_faces, MODES * part_rhs)
        outgoing = jnp.dot(send_table, payload, preferred_element_type=jnp.float32).astype(
            jnp.bfloat16
        )
        blocks = outgoing.reshape(neighbours, capacity, -1)
        arrivals = []
        for link in range(neighbours):
            arrivals.append(passed_along(blocks[link], SUB, link - REACH))
        arrived = jnp.concatenate(arrivals, axis=0)
        mortar_sums = jnp.dot(owner_table, arrived, preferred_element_type=jnp.float32)
        shaped = mortar_sums.reshape(MORT_OWN, MODES, part_rhs) / divisor[:, None, None]
        shaped = shaped * keep_mask[:, :, None]
        averages = shaped.reshape(MORT_OWN, MODES * part_rhs).astype(jnp.bfloat16)
        replies = lax.dot_general(
            owner_table, averages, contract_first, preferred_element_type=jnp.float32
        ).astype(jnp.bfloat16)
        reply_blocks = replies.reshape(neighbours, capacity, -1)
        answers = []
        for link in range(neighbours):
            answers.append(passed_along(reply_blocks[link], SUB, REACH - link))
        answered = jnp.concatenate(answers, axis=0)
        own_back = lax.dot_general(
            send_table, answered, contract_first, preferred_element_type=jnp.float32
        ).astype(jnp.bfloat16)
        returned = lax.all_to_all(
            own_back.reshape(all_faces, MODES, part_rhs),
            "grp",
            split_axis=0,
            concat_axis=2,
            tiled=True,
        )
        lifted = jnp.einsum(
            "fmp,fmr->fpr", tables, returned, preferred_element_type=jnp.float32
        ).reshape(own_rows, -1)
        partial_value = jnp.dot(coarse_wide, lifted, precision=highest)
        summed = taken_together(partial_value, "grp")
        spread = lax.dot_general(corner_hot, summed, contract_first, precision=highest)
        vertex = sum_by_parts(spread, (("sub_0", "sub_1"), "sub_2"))
        picked = jnp.dot(corner_hot, vertex, precision=highest)
        coarse_corr = lax.dot_general(coarse_wide, picked, contract_first, precision=highest)
        traces = traces - relax_weight * lifted - coarse_weight * coarse_corr
    return traces[None]


def solution(mesh):
    finer = Mesh(
        mesh.devices.reshape(8, 8, 2, mesh.shape["grp"]), ("sub_0", "sub_1", "sub_2", "grp")
    )
    placed = (
        P(SUB, "grp", None),
        P(SUB, "grp", None),
        P(SUB, "grp", None),
        P(SUB, "grp", None),
        P(SUB, None, "grp"),
        P(),
        P(),
        P(),
        P(),
        P(),
    )
    return jax.shard_map(
        body, mesh=finer, in_specs=placed, out_specs=P(SUB, "grp", None), check_vma=False
    )
```

profile of v0, /device:TPU:1, one launch (start us, length us, event | category | flops | bytes accessed | tf_op | source)
XLA Modules:
  0.0 286.5 jit_solution(6291105881597627095)
XLA Ops:
  0.0 1.2 bitcast_convert_fusion
  2.2 5.0 %all-to-all-start = ((bf16[4,512,192]{1,2,0:T(8,128)(2,1)}), bf16[4,512,192]{1,2,0:T(8,128)(2,1)S(1)}, u32[]{:S(2)}, u32[]{:S(2)}) async-start(bf16[4,512,192]{1,2,0:T(8,128)(2,1)} %broadcast_in_dim.48), calls=%async_computation | async-start | bytes 1572864 | tf_op jit(solution)/shard_map/all_to_all | solution.py:29
  9.8 1.4 broadcast_select_fusion
  11.8 1.3 fusion.68
  13.3 1.4 gather_fusion.4
  15.4 1.0 reshape_squeeze.3
  20.9 1.0 reshape.341
  21.9 4.2 %all-to-all-start.1 = ((bf16[4,2,12288]{2,1,0:T(2,128)(2,1)}), bf16[4,2,12288]{2,1,0:T(2,128)(2,1)S(1)}, u32[]{:S(2)}, u32[]{:S(2)}) async-start(bf16[4,2,12288]{2,1,0:T(2,128)(2,1)} %reshape.341), calls=%async_computation.1 | async-start | bytes 393216 | tf_op jit(solution)/shard_map/all_to_all | solution.py:160
  26.2 5.1 %all-to-all-done.1 = bf16[4,2,12288]{2,1,0:T(2,128)(2,1)S(1)} async-done(((bf16[4,2,12288]{2,1,0:T(2,128)(2,1)}), bf16[4,2,12288]{2,1,0:T(2,128)(2,1)S(1)}, u32[]{:S(2)}, u32[]{:S(2)}) %all-to-all-start.1) | async-done | bytes 196640 | tf_op jit(solution)/shard_map/all_to_all | solution.py:160
  33.0 13.6 %collective-permute-start = (bf16[8,3072]{1,0:T(8,128)(2,1)S(1)}, bf16[8,3072]{1,0:T(8,128)(2,1)S(1)}, u32[]{:S(2)}, u32[]{:S(2)}) collective-permute-start(bf16[8,3072]{1,0:T(8,128)(2,1)S(1)} %get-tuple-element.28), channel_id=1, source_target_pairs={{0,504},{4,508},{8,0},{12,4},{16,8},{20,12},{24,16},{28,20},{32,24... | collective-permute-start | bytes 147464 | tf_op jit(solution)/shard_map/ppermute | solution.py:39
  46.7 1.9 collective-permute-start.4
  48.6 1.9 collective-permute-start.3
  50.6 4.9 %collective-permute-start.1 = (bf16[8,3072]{1,0:T(8,128)(2,1)S(1)}, bf16[8,3072]{1,0:T(8,128)(2,1)S(1)}, u32[]{:S(2)}, u32[]{:S(2)}) collective-permute-start(bf16[8,3072]{1,0:T(8,128)(2,1)S(1)} %get-tuple-element.27), channel_id=1, source_target_pairs={{0,508},{4,0},{8,4},{12,8},{16,12},{20,16},{24,20},{28,24},{32,28}... | collective-permute-start | bytes 147464 | tf_op jit(solution)/shard_map/ppermute | solution.py:39
  58.5 1.9 collective-permute-start.5
  60.4 12.5 %collective-permute-start.9 = (bf16[8,3072]{1,0:T(8,128)(2,1)S(1)}, bf16[8,3072]{1,0:T(8,128)(2,1)S(1)}, u32[]{:S(2)}, u32[]{:S(2)}) collective-permute-start(bf16[8,3072]{1,0:T(8,128)(2,1)S(1)} %get-tuple-element.19), channel_id=1, source_target_pairs={{0,504},{4,508},{8,0},{12,4},{16,8},{20,12},{24,16},{28,20},{32,24... | collective-permute-start | bytes 147464 | tf_op jit(solution)/shard_map/ppermute | solution.py:39
  72.9 2.5 collective-permute-start.8
  75.5 3.0 %collective-permute-start.6 = (bf16[8,3072]{1,0:T(8,128)(2,1)S(1)}, bf16[8,3072]{1,0:T(8,128)(2,1)S(1)}, u32[]{:S(2)}, u32[]{:S(2)}) collective-permute-start(bf16[8,3072]{1,0:T(8,128)(2,1)S(1)} %get-tuple-element.22), channel_id=1, source_target_pairs={{0,4},{4,8},{8,12},{12,16},{16,20},{20,24},{24,28},{28,32},{32,36}... | collective-permute-start | bytes 147464 | tf_op jit(solution)/shard_map/ppermute | solution.py:39
  78.5 1.1 collective-permute-done.6
  81.8 3.4 %all-to-all-start.2 = ((bf16[4,2,12288]{2,1,0:T(2,128)(2,1)}), bf16[4,2,12288]{2,1,0:T(2,128)(2,1)S(1)}, u32[]{:S(2)}, u32[]{:S(2)}) async-start(bf16[4,2,12288]{2,1,0:T(2,128)(2,1)} %reshape.343), calls=%async_computation.2 | async-start | bytes 393216 | tf_op jit(solution)/shard_map/all_to_all | solution.py:186
  86.7 3.6 %all-to-all-done.2 = bf16[4,2,12288]{2,1,0:T(2,128)(2,1)S(1)} async-done(((bf16[4,2,12288]{2,1,0:T(2,128)(2,1)}), bf16[4,2,12288]{2,1,0:T(2,128)(2,1)S(1)}, u32[]{:S(2)}, u32[]{:S(2)}) %all-to-all-start.2) | async-done | bytes 196640 | tf_op jit(solution)/shard_map/all_to_all | solution.py:186
  92.0 3.3 %all-to-all-start.3 = ((f32[4,8,192]{2,1,0:T(8,128)}), f32[4,8,192]{2,1,0:T(8,128)S(1)}, u32[]{:S(2)}, u32[]{:S(2)}) async-start(f32[4,8,192]{2,1,0:T(8,128)} %broadcast_in_dim.83), calls=%async_computation.3 | async-start | bytes 65536 | tf_op jit(solution)/shard_map/all_to_all | solution.py:29
  95.9 3.6 %all-to-all-done.3 = f32[4,8,192]{2,1,0:T(8,128)S(1)} async-done(((f32[4,8,192]{2,1,0:T(8,128)}), f32[4,8,192]{2,1,0:T(8,128)S(1)}, u32[]{:S(2)}, u32[]{:S(2)}) %all-to-all-start.3) | async-done | bytes 24608 | tf_op jit(solution)/shard_map/all_to_all | solution.py:29
  99.9 11.6 %all_to_all.126 = f32[2,64,2,192]{3,1,2,0:T(8,128)S(1)} all-to-all(f32[2,64,2,192]{3,1,2,0:T(8,128)S(1)} %convolution_bitcast_fusion.1), channel_id=1, replica_groups=mesh['sub_0'=8,'sub_1'=8,'sub_2'=2,'grp'=4] {'sub_2'}, dimensions={0} | all-to-all | bytes 393216 | tf_op jit(solution)/shard_map/all_to_all | solution.py:64
  111.7 15.4 %all_to_all.127 = f32[64,2,192]{2,1,0:T(2,128)S(1)} all-to-all(f32[64,2,192]{2,1,0:T(2,128)S(1)} %copy.170), channel_id=1, replica_groups=mesh['sub_0'=8,'sub_1'=8,'sub_2'=2,'grp'=4] {'sub_0','sub_1'}, dimensions={0} | all-to-all | bytes 196608 | tf_op jit(solution)/shard_map/all_to_all | solution.py:72
  127.9 5.5 %all-to-all-start.6 = ((f32[64,2,192]{2,1,0:T(2,128)}), f32[64,2,192]{2,1,0:T(2,128)}, u32[]{:S(2)}, u32[]{:S(2)}) async-start(f32[64,2,192]{2,1,0:T(2,128)} %broadcast_in_dim.84), calls=%async_computation.6 | async-start | bytes 262144 | tf_op jit(solution)/shard_map/all_to_all | solution.py:29
  133.6 11.2 %all-to-all-done.6 = f32[64,2,192]{2,1,0:T(2,128)} async-done(((f32[64,2,192]{2,1,0:T(2,128)}), f32[64,2,192]{2,1,0:T(2,128)}, u32[]{:S(2)}, u32[]{:S(2)}) %all-to-all-start.6) | async-done | bytes 98336 | tf_op jit(solution)/shard_map/all_to_all | solution.py:29
  145.8 6.8 %all_to_all.128 = f32[2,64,2,192]{3,2,1,0:T(2,128)S(1)} all-to-all(f32[2,64,2,192]{3,2,1,0:T(2,128)S(1)} %broadcast_in_dim.85), channel_id=1, replica_groups=mesh['sub_0'=8,'sub_1'=8,'sub_2'=2,'grp'=4] {'sub_2'}, dimensions={0} | all-to-all | bytes 393216 | tf_op jit(solution)/shard_map/all_to_all | solution.py:29
  153.0 1.2 fusion.73
  154.2 14.6 %all_to_all.129 = bf16[4,512,192]{1,2,0:T(8,128)(2,1)S(1)} all-to-all(bf16[4,512,192]{1,2,0:T(8,128)(2,1)S(1)} %broadcast_in_dim.86), channel_id=1, replica_groups=mesh['sub_0'=8,'sub_1'=8,'sub_2'=2,'grp'=4] {'grp'}, dimensions={0} | all-to-all | bytes 1572864 | tf_op jit(solution)/shard_map/all_to_all | solution.py:29
  170.7 7.5 %all_to_all.130 = bf16[4,2,12288]{2,1,0:T(2,128)(2,1)S(1)} all-to-all(bf16[4,2,12288]{2,1,0:T(2,128)(2,1)S(1)} %reshape.345), channel_id=1, replica_groups=mesh['sub_0'=8,'sub_1'=8,'sub_2'=2,'grp'=4] {'grp'}, dimensions={0} | all-to-all | bytes 393216 | tf_op jit(solution)/shard_map/all_to_all | solution.py:160
  179.9 2.2 collective-permute-start.10
  182.1 3.1 %collective-permute-start.14 = (bf16[8,3072]{1,0:T(8,128)(2,1)S(1)}, bf16[8,3072]{1,0:T(8,128)(2,1)S(1)}, u32[]{:S(2)}, u32[]{:S(2)}) collective-permute-start(bf16[8,3072]{1,0:T(8,128)(2,1)S(1)} %get-tuple-element.14), channel_id=1, source_target_pairs={{0,8},{4,12},{8,16},{12,20},{16,24},{20,28},{24,32},{28,36},{32,40... | collective-permute-start | bytes 147464 | tf_op jit(solution)/shard_map/ppermute | solution.py:39
  185.2 5.1 %collective-permute-start.13 = (bf16[8,3072]{1,0:T(8,128)(2,1)S(1)}, bf16[8,3072]{1,0:T(8,128)(2,1)S(1)}, u32[]{:S(2)}, u32[]{:S(2)}) collective-permute-start(bf16[8,3072]{1,0:T(8,128)(2,1)S(1)} %get-tuple-element.15), channel_id=1, source_target_pairs={{0,4},{4,8},{8,12},{12,16},{16,20},{20,24},{24,28},{28,32},{32,36}... | collective-permute-start | bytes 147464 | tf_op jit(solution)/shard_map/ppermute | solution.py:39
  190.3 1.9 collective-permute-start.11
  192.3 3.8 %collective-permute-done.11 = bf16[8,3072]{1,0:T(8,128)(2,1)S(1)} collective-permute-done((bf16[8,3072]{1,0:T(8,128)(2,1)S(1)}, bf16[8,3072]{1,0:T(8,128)(2,1)S(1)}, u32[]{:S(2)}, u32[]{:S(2)}) %collective-permute-start.11) | collective-permute-done | bytes 49184 | tf_op jit(solution)/shard_map/ppermute | solution.py:39
  198.9 2.0 collective-permute-start.15
  200.9 9.2 %collective-permute-start.19 = (bf16[8,3072]{1,0:T(8,128)(2,1)S(1)}, bf16[8,3072]{1,0:T(8,128)(2,1)S(1)}, u32[]{:S(2)}, u32[]{:S(2)}) collective-permute-start(bf16[8,3072]{1,0:T(8,128)(2,1)S(1)} %get-tuple-element.9), channel_id=1, source_target_pairs={{0,504},{4,508},{8,0},{12,4},{16,8},{20,12},{24,16},{28,20},{32,24... | collective-permute-start | bytes 147464 | tf_op jit(solution)/shard_map/ppermute | solution.py:39
  210.1 2.5 collective-permute-start.18
  212.7 3.0 %collective-permute-start.16 = (bf16[8,3072]{1,0:T(8,128)(2,1)S(1)}, bf16[8,3072]{1,0:T(8,128)(2,1)S(1)}, u32[]{:S(2)}, u32[]{:S(2)}) collective-permute-start(bf16[8,3072]{1,0:T(8,128)(2,1)S(1)} %get-tuple-element.12), channel_id=1, source_target_pairs={{0,4},{4,8},{8,12},{12,16},{16,20},{20,24},{24,28},{28,32},{32,36}... | collective-permute-start | bytes 147464 | tf_op jit(solution)/shard_map/ppermute | solution.py:39
  215.7 1.1 collective-permute-done.16
  218.3 7.5 %all_to_all.131 = bf16[4,2,12288]{2,1,0:T(2,128)(2,1)S(1)} all-to-all(bf16[4,2,12288]{2,1,0:T(2,128)(2,1)S(1)} %reshape.347), channel_id=1, replica_groups=mesh['sub_0'=8,'sub_1'=8,'sub_2'=2,'grp'=4] {'grp'}, dimensions={0} | all-to-all | bytes 393216 | tf_op jit(solution)/shard_map/all_to_all | solution.py:186
  226.9 6.7 %all_to_all.132 = f32[4,8,192]{2,1,0:T(8,128)S(1)} all-to-all(f32[4,8,192]{2,1,0:T(8,128)S(1)} %broadcast_in_dim.87), channel_id=1, replica_groups=mesh['sub_0'=8,'sub_1'=8,'sub_2'=2,'grp'=4] {'grp'}, dimensions={0} | all-to-all | bytes 49152 | tf_op jit(solution)/shard_map/all_to_all | solution.py:29
  233.9 11.6 %all_to_all.133 = f32[2,64,2,192]{3,1,2,0:T(8,128)S(1)} all-to-all(f32[2,64,2,192]{3,1,2,0:T(8,128)S(1)} %convolution_bitcast_fusion), channel_id=1, replica_groups=mesh['sub_0'=8,'sub_1'=8,'sub_2'=2,'grp'=4] {'sub_2'}, dimensions={0} | all-to-all | bytes 393216 | tf_op jit(solution)/shard_map/all_to_all | solution.py:64
  245.7 15.4 %all_to_all.134 = f32[64,2,192]{2,1,0:T(2,128)S(1)} all-to-all(f32[64,2,192]{2,1,0:T(2,128)S(1)} %copy.185), channel_id=1, replica_groups=mesh['sub_0'=8,'sub_1'=8,'sub_2'=2,'grp'=4] {'sub_0','sub_1'}, dimensions={0} | all-to-all | bytes 196608 | tf_op jit(solution)/shard_map/all_to_all | solution.py:72
  261.9 4.6 %all-to-all-start.14 = ((f32[64,2,192]{2,1,0:T(2,128)}), f32[64,2,192]{2,1,0:T(2,128)S(1)}, u32[]{:S(2)}, u32[]{:S(2)}) async-start(f32[64,2,192]{2,1,0:T(2,128)} %broadcast_in_dim.88), calls=%async_computation.14 | async-start | bytes 262144 | tf_op jit(solution)/shard_map/all_to_all | solution.py:29
  266.7 11.4 %all-to-all-done.14 = f32[64,2,192]{2,1,0:T(2,128)S(1)} async-done(((f32[64,2,192]{2,1,0:T(2,128)}), f32[64,2,192]{2,1,0:T(2,128)S(1)}, u32[]{:S(2)}, u32[]{:S(2)}) %all-to-all-start.14) | async-done | bytes 98336 | tf_op jit(solution)/shard_map/all_to_all | solution.py:29
  278.2 6.7 %all_to_all.135 = f32[2,64,2,192]{3,2,1,0:T(2,128)S(1)} all-to-all(f32[2,64,2,192]{3,2,1,0:T(2,128)S(1)} %broadcast_in_dim.89), channel_id=1, replica_groups=mesh['sub_0'=8,'sub_1'=8,'sub_2'=2,'grp'=4] {'sub_2'}, dimensions={0} | all-to-all | bytes 393216 | tf_op jit(solution)/shard_map/all_to_all | solution.py:29
  285.3 1.2 fusion.6
  (194 shorter events, 33.6 us)
Async XLA Ops:
  0.0 19.4 %copy-start = (bf16[1,512,2048]{2,1,0:T(8,128)(2,1)S(1)}, bf16[1,512,2048]{2,1,0:T(8,128)(2,1)}, u32[]{:S(2)}) copy-start(bf16[1,512,2048]{2,1,0:T(8,128)(2,1)} %param.14) | copy-start | bytes 6291460
  0.0 7.7 %copy-start.22 = (s32[128]{0:T(128)S(1)}, s32[128]{0:T(128)}, u32[]{:S(2)}) copy-start(s32[128]{0:T(128)} %param.22) | copy-start | bytes 1540
  0.0 8.2 %copy-start.8 = (s32[128,32,1]{0,2,1:T(1,128)S(1)}, s32[128,32,1]{0,2,1:T(1,128)}, u32[]{:S(2)}) copy-start(s32[128,32,1]{0,2,1:T(1,128)} %param.19) | copy-start | bytes 49156
  0.0 8.3 %copy-start.9 = (s32[128,32]{0,1:T(8,128)S(1)}, s32[128,32]{0,1:T(8,128)}, u32[]{:S(2)}) copy-start(s32[128,32]{0,1:T(8,128)} %param.20) | copy-start | bytes 49156
  2.2 14.3 %copy-start.12 = (s32[128,16]{0,1:T(8,128)S(1)}, s32[128,16]{0,1:T(8,128)}, u32[]{:S(2)}) copy-start(s32[128,16]{0,1:T(8,128)} %param.21) | copy-start | bytes 24580
  2.2 17.1 %all-to-all-start = ((bf16[4,512,192]{1,2,0:T(8,128)(2,1)}), bf16[4,512,192]{1,2,0:T(8,128)(2,1)S(1)}, u32[]{:S(2)}, u32[]{:S(2)}) async-start(bf16[4,512,192]{1,2,0:T(8,128)(2,1)} %broadcast_in_dim.48), calls=%async_computation | async-start | bytes 1572864 | tf_op jit(solution)/shard_map/all_to_all | solution.py:29
  7.1 12.3 %copy-start.3 = (f32[1,512,192]{1,2,0:T(8,128)S(1)}, f32[1,512,192]{1,2,0:T(8,128)}, u32[]{:S(2)}) copy-start(f32[1,512,192]{1,2,0:T(8,128)} %param.15) | copy-start | bytes 1179652
  8.5 6.2 %copy-start.14 = (s32[1024]{0:T(1024)}, s32[1024]{0:T(1024)S(1)}, u32[]{:S(2)}) copy-start(s32[1024]{0:T(1024)S(1)} %get-tuple-element.37) | copy-start | bytes 12292
  19.3 38.9 %copy-start.6 = (bf16[5,8,16]{2,1,0:T(8,128)(2,1)}, bf16[5,8,16]{2,1,0:T(8,128)(2,1)S(1)}, u32[]{:S(2)}) copy-start(bf16[5,8,16]{2,1,0:T(8,128)(2,1)S(1)} %convolution_convert_fusion.8) | copy-start | bytes 3844
  20.3 5.9 %copy-start.17 = (s32[16]{0:T(128)S(1)}, s32[16]{0:T(128)}, u32[]{:S(2)}) copy-start(s32[16]{0:T(128)} %dynamic-slice_reduce_fusion) | copy-start | bytes 196
  20.3 5.9 %copy-start.20 = (s32[64]{0:T(128)S(1)}, s32[64]{0:T(128)}, u32[]{:S(2)}) copy-start(s32[64]{0:T(128)} %get-tuple-element.35) | copy-start | bytes 772
  20.9 25.7 %copy-start.18 = (pred[5,32]{1,0:T(8,128)(4,1)S(1)}, pred[5,32]{1,0:T(8,128)(4,1)}, u32[]{:S(2)}) copy-start(pred[5,32]{1,0:T(8,128)(4,1)} %get-tuple-element.8) | copy-start | bytes 484
  21.9 9.4 %all-to-all-start.1 = ((bf16[4,2,12288]{2,1,0:T(2,128)(2,1)}), bf16[4,2,12288]{2,1,0:T(2,128)(2,1)S(1)}, u32[]{:S(2)}, u32[]{:S(2)}) async-start(bf16[4,2,12288]{2,1,0:T(2,128)(2,1)} %reshape.341), calls=%async_computation.1 | async-start | bytes 393216 | tf_op jit(solution)/shard_map/all_to_all | solution.py:160
  26.2 55.6 %copy-start.13 = (f32[16,64]{1,0:T(8,128)}, f32[16,64]{1,0:T(8,128)S(1)}, u32[]{:S(2)}) copy-start(f32[16,64]{1,0:T(8,128)S(1)} %and_convert_fusion) | copy-start | bytes 12292
  26.2 53.5 %copy-start.10 = (s32[32]{0:T(128)}, s32[32]{0:T(128)S(1)}, u32[]{:S(2)}) copy-start(s32[32]{0:T(128)S(1)} %fusion.66) | copy-start | bytes 388
  33.0 22.4 %collective-permute-start = (bf16[8,3072]{1,0:T(8,128)(2,1)S(1)}, bf16[8,3072]{1,0:T(8,128)(2,1)S(1)}, u32[]{:S(2)}, u32[]{:S(2)}) collective-permute-start(bf16[8,3072]{1,0:T(8,128)(2,1)S(1)} %get-tuple-element.28), channel_id=1, source_target_pairs={{0,504},{4,508},{8,0},{12,4},{16,8},{20,12},{24,16},{28,20},{32,24... | collective-permute-start | bytes 147464 | tf_op jit(solution)/shard_map/ppermute | solution.py:39
  46.7 11.2 %copy-start.23 = (f32[16]{0:T(128)}, f32[16]{0:T(128)S(1)}, u32[]{:S(2)}) copy-start(f32[16]{0:T(128)S(1)} %fusion.30) | copy-start | bytes 196
  46.7 9.6 %collective-permute-start.4 = (bf16[8,3072]{1,0:T(8,128)(2,1)S(1)}, bf16[8,3072]{1,0:T(8,128)(2,1)S(1)}, u32[]{:S(2)}, u32[]{:S(2)}) collective-permute-start(bf16[8,3072]{1,0:T(8,128)(2,1)S(1)} %get-tuple-element.24), channel_id=1, source_target_pairs={{0,8},{4,12},{8,16},{12,20},{16,24},{20,28},{24,32},{28,36},{32,40... | collective-permute-start | bytes 147464 | tf_op jit(solution)/shard_map/ppermute | solution.py:39
  48.6 7.7 %collective-permute-start.3 = (bf16[8,3072]{1,0:T(8,128)(2,1)S(1)}, bf16[8,3072]{1,0:T(8,128)(2,1)S(1)}, u32[]{:S(2)}, u32[]{:S(2)}) collective-permute-start(bf16[8,3072]{1,0:T(8,128)(2,1)S(1)} %get-tuple-element.25), channel_id=1, source_target_pairs={{0,4},{4,8},{8,12},{12,16},{16,20},{20,24},{24,28},{28,32},{32,36}... | collective-permute-start | bytes 147464 | tf_op jit(solution)/shard_map/ppermute | solution.py:39
  50.5 5.7 %collective-permute-start.2 = (bf16[8,3072]{1,0:T(8,128)(2,1)S(1)}, bf16[8,3072]{1,0:T(8,128)(2,1)S(1)}, u32[]{:S(2)}, u32[]{:S(2)}) collective-permute-start(bf16[8,3072]{1,0:T(8,128)(2,1)S(1)} %get-tuple-element.26), channel_id=1, source_target_pairs={{0,0},{4,4},{8,8},{12,12},{16,16},{20,20},{24,24},{28,28},{32,32},... | collective-permute-start | bytes 147464 | tf_op jit(solution)/shard_map/ppermute | solution.py:39
  50.6 5.7 %collective-permute-start.1 = (bf16[8,3072]{1,0:T(8,128)(2,1)S(1)}, bf16[8,3072]{1,0:T(8,128)(2,1)S(1)}, u32[]{:S(2)}, u32[]{:S(2)}) collective-permute-start(bf16[8,3072]{1,0:T(8,128)(2,1)S(1)} %get-tuple-element.27), channel_id=1, source_target_pairs={{0,508},{4,0},{8,4},{12,8},{16,12},{20,16},{24,20},{28,24},{32,28}... | collective-permute-start | bytes 147464 | tf_op jit(solution)/shard_map/ppermute | solution.py:39
  58.4 26.8 %copy-start.19 = (pred[128]{0:T(512)(128)(4,1)S(1)}, pred[128]{0:T(512)(128)(4,1)}, u32[]{:S(2)}) copy-start(pred[128]{0:T(512)(128)(4,1)} %compare_and_fusion.1) | copy-start | bytes 388
  58.4 27.4 %copy-start.16 = (s32[128,8]{0,1:T(8,128)S(1)}, s32[128,8]{0,1:T(8,128)}, u32[]{:S(2)}) copy-start(s32[128,8]{0,1:T(8,128)} %param.23) | copy-start | bytes 12292
  58.5 20.1 %collective-permute-start.5 = (bf16[8,3072]{1,0:T(8,128)(2,1)S(1)}, bf16[8,3072]{1,0:T(8,128)(2,1)S(1)}, u32[]{:S(2)}, u32[]{:S(2)}) collective-permute-start(bf16[8,3072]{1,0:T(8,128)(2,1)S(1)} %get-tuple-element.23), channel_id=1, source_target_pairs={{0,8},{4,12},{8,16},{12,20},{16,24},{20,28},{24,32},{28,36},{32,40... | collective-permute-start | bytes 147464 | tf_op jit(solution)/shard_map/ppermute | solution.py:39
  60.4 19.3 %collective-permute-start.9 = (bf16[8,3072]{1,0:T(8,128)(2,1)S(1)}, bf16[8,3072]{1,0:T(8,128)(2,1)S(1)}, u32[]{:S(2)}, u32[]{:S(2)}) collective-permute-start(bf16[8,3072]{1,0:T(8,128)(2,1)S(1)} %get-tuple-element.19), channel_id=1, source_target_pairs={{0,504},{4,508},{8,0},{12,4},{16,8},{20,12},{24,16},{28,20},{32,24... | collective-permute-start | bytes 147464 | tf_op jit(solution)/shard_map/ppermute | solution.py:39
  72.9 6.8 %collective-permute-start.8 = (bf16[8,3072]{1,0:T(8,128)(2,1)S(1)}, bf16[8,3072]{1,0:T(8,128)(2,1)S(1)}, u32[]{:S(2)}, u32[]{:S(2)}) collective-permute-start(bf16[8,3072]{1,0:T(8,128)(2,1)S(1)} %get-tuple-element.20), channel_id=1, source_target_pairs={{0,508},{4,0},{8,4},{12,8},{16,12},{20,16},{24,20},{28,24},{32,28}... | collective-permute-start | bytes 147464 | tf_op jit(solution)/shard_map/ppermute | solution.py:39
  75.5 4.2 %collective-permute-start.7 = (bf16[8,3072]{1,0:T(8,128)(2,1)S(1)}, bf16[8,3072]{1,0:T(8,128)(2,1)S(1)}, u32[]{:S(2)}, u32[]{:S(2)}) collective-permute-start(bf16[8,3072]{1,0:T(8,128)(2,1)S(1)} %get-tuple-element.21), channel_id=1, source_target_pairs={{0,0},{4,4},{8,8},{12,12},{16,16},{20,20},{24,24},{28,28},{32,32},... | collective-permute-start | bytes 147464 | tf_op jit(solution)/shard_map/ppermute | solution.py:39
  75.5 4.2 %collective-permute-start.6 = (bf16[8,3072]{1,0:T(8,128)(2,1)S(1)}, bf16[8,3072]{1,0:T(8,128)(2,1)S(1)}, u32[]{:S(2)}, u32[]{:S(2)}) collective-permute-start(bf16[8,3072]{1,0:T(8,128)(2,1)S(1)} %get-tuple-element.22), channel_id=1, source_target_pairs={{0,4},{4,8},{8,12},{12,16},{16,20},{20,24},{24,28},{28,32},{32,36}... | collective-permute-start | bytes 147464 | tf_op jit(solution)/shard_map/ppermute | solution.py:39
  80.8 10.2 %copy-start.5 = (bf16[1,8,512]{2,1,0:T(8,128)(2,1)S(1)}, bf16[1,8,512]{2,1,0:T(8,128)(2,1)}, u32[]{:S(2)}) copy-start(bf16[1,8,512]{2,1,0:T(8,128)(2,1)} %param.18) | copy-start | bytes 24580
  81.8 8.5 %all-to-all-start.2 = ((bf16[4,2,12288]{2,1,0:T(2,128)(2,1)}), bf16[4,2,12288]{2,1,0:T(2,128)(2,1)S(1)}, u32[]{:S(2)}, u32[]{:S(2)}) async-start(bf16[4,2,12288]{2,1,0:T(2,128)(2,1)} %reshape.343), calls=%async_computation.2 | async-start | bytes 393216 | tf_op jit(solution)/shard_map/all_to_all | solution.py:186
  92.0 7.5 %all-to-all-start.3 = ((f32[4,8,192]{2,1,0:T(8,128)}), f32[4,8,192]{2,1,0:T(8,128)S(1)}, u32[]{:S(2)}, u32[]{:S(2)}) async-start(f32[4,8,192]{2,1,0:T(8,128)} %broadcast_in_dim.83), calls=%async_computation.3 | async-start | bytes 65536 | tf_op jit(solution)/shard_map/all_to_all | solution.py:29
  111.6 41.4 %copy-start.1 = (f32[1,512,192]{1,2,0:T(8,128)S(1)}, f32[1,512,192]{1,2,0:T(8,128)}, u32[]{:S(2)}) copy-start(f32[1,512,192]{1,2,0:T(8,128)} %param.16) | copy-start | bytes 1179652
  127.9 16.9 %all-to-all-start.6 = ((f32[64,2,192]{2,1,0:T(2,128)}), f32[64,2,192]{2,1,0:T(2,128)}, u32[]{:S(2)}, u32[]{:S(2)}) async-start(f32[64,2,192]{2,1,0:T(2,128)} %broadcast_in_dim.84), calls=%async_computation.6 | async-start | bytes 262144 | tf_op jit(solution)/shard_map/all_to_all | solution.py:29
  154.1 14.8 %copy-start.4 = (f32[1,512,192]{1,2,0:T(8,128)S(1)}, f32[1,512,192]{1,2,0:T(8,128)}, u32[]{:S(2)}) copy-start(f32[1,512,192]{1,2,0:T(8,128)} %param.15) | copy-start | bytes 1179652
  170.1 9.5 %copy-start.11 = (s32[32]{0:T(128)S(1)}, s32[32]{0:T(128)}, u32[]{:S(2)}) copy-start(s32[32]{0:T(128)} %copy-done.10) | copy-start | bytes 388
  178.9 18.2 %copy-start.7 = (bf16[5,8,16]{2,1,0:T(8,128)(2,1)S(1)}, bf16[5,8,16]{2,1,0:T(8,128)(2,1)}, u32[]{:S(2)}) copy-start(bf16[5,8,16]{2,1,0:T(8,128)(2,1)} %copy-done.6) | copy-start | bytes 3844
  179.9 12.3 %collective-permute-start.10 = (bf16[8,3072]{1,0:T(8,128)(2,1)S(1)}, bf16[8,3072]{1,0:T(8,128)(2,1)S(1)}, u32[]{:S(2)}, u32[]{:S(2)}) collective-permute-start(bf16[8,3072]{1,0:T(8,128)(2,1)S(1)} %get-tuple-element.18), channel_id=1, source_target_pairs={{0,504},{4,508},{8,0},{12,4},{16,8},{20,12},{24,16},{28,20},{32,24... | collective-permute-start | bytes 147464 | tf_op jit(solution)/shard_map/ppermute | solution.py:39
  182.1 14.0 %collective-permute-start.14 = (bf16[8,3072]{1,0:T(8,128)(2,1)S(1)}, bf16[8,3072]{1,0:T(8,128)(2,1)S(1)}, u32[]{:S(2)}, u32[]{:S(2)}) collective-permute-start(bf16[8,3072]{1,0:T(8,128)(2,1)S(1)} %get-tuple-element.14), channel_id=1, source_target_pairs={{0,8},{4,12},{8,16},{12,20},{16,24},{20,28},{24,32},{28,36},{32,40... | collective-permute-start | bytes 147464 | tf_op jit(solution)/shard_map/ppermute | solution.py:39
  185.2 10.8 %collective-permute-start.13 = (bf16[8,3072]{1,0:T(8,128)(2,1)S(1)}, bf16[8,3072]{1,0:T(8,128)(2,1)S(1)}, u32[]{:S(2)}, u32[]{:S(2)}) collective-permute-start(bf16[8,3072]{1,0:T(8,128)(2,1)S(1)} %get-tuple-element.15), channel_id=1, source_target_pairs={{0,4},{4,8},{8,12},{12,16},{16,20},{20,24},{24,28},{28,32},{32,36}... | collective-permute-start | bytes 147464 | tf_op jit(solution)/shard_map/ppermute | solution.py:39
  190.3 5.7 %collective-permute-start.12 = (bf16[8,3072]{1,0:T(8,128)(2,1)S(1)}, bf16[8,3072]{1,0:T(8,128)(2,1)S(1)}, u32[]{:S(2)}, u32[]{:S(2)}) collective-permute-start(bf16[8,3072]{1,0:T(8,128)(2,1)S(1)} %get-tuple-element.16), channel_id=1, source_target_pairs={{0,0},{4,4},{8,8},{12,12},{16,16},{20,20},{24,24},{28,28},{32,32},... | collective-permute-start | bytes 147464 | tf_op jit(solution)/shard_map/ppermute | solution.py:39
  190.3 5.7 %collective-permute-start.11 = (bf16[8,3072]{1,0:T(8,128)(2,1)S(1)}, bf16[8,3072]{1,0:T(8,128)(2,1)S(1)}, u32[]{:S(2)}, u32[]{:S(2)}) collective-permute-start(bf16[8,3072]{1,0:T(8,128)(2,1)S(1)} %get-tuple-element.17), channel_id=1, source_target_pairs={{0,508},{4,0},{8,4},{12,8},{16,12},{20,16},{24,20},{28,24},{32,28}... | collective-permute-start | bytes 147464 | tf_op jit(solution)/shard_map/ppermute | solution.py:39
  198.9 16.8 %collective-permute-start.15 = (bf16[8,3072]{1,0:T(8,128)(2,1)S(1)}, bf16[8,3072]{1,0:T(8,128)(2,1)S(1)}, u32[]{:S(2)}, u32[]{:S(2)}) collective-permute-start(bf16[8,3072]{1,0:T(8,128)(2,1)S(1)} %get-tuple-element.13), channel_id=1, source_target_pairs={{0,8},{4,12},{8,16},{12,20},{16,24},{20,28},{24,32},{28,36},{32,40... | collective-permute-start | bytes 147464 | tf_op jit(solution)/shard_map/ppermute | solution.py:39
  200.9 16.0 %collective-permute-start.19 = (bf16[8,3072]{1,0:T(8,128)(2,1)S(1)}, bf16[8,3072]{1,0:T(8,128)(2,1)S(1)}, u32[]{:S(2)}, u32[]{:S(2)}) collective-permute-start(bf16[8,3072]{1,0:T(8,128)(2,1)S(1)} %get-tuple-element.9), channel_id=1, source_target_pairs={{0,504},{4,508},{8,0},{12,4},{16,8},{20,12},{24,16},{28,20},{32,24... | collective-permute-start | bytes 147464 | tf_op jit(solution)/shard_map/ppermute | solution.py:39
  210.1 6.8 %collective-permute-start.18 = (bf16[8,3072]{1,0:T(8,128)(2,1)S(1)}, bf16[8,3072]{1,0:T(8,128)(2,1)S(1)}, u32[]{:S(2)}, u32[]{:S(2)}) collective-permute-start(bf16[8,3072]{1,0:T(8,128)(2,1)S(1)} %get-tuple-element.10), channel_id=1, source_target_pairs={{0,508},{4,0},{8,4},{12,8},{16,12},{20,16},{24,20},{28,24},{32,28}... | collective-permute-start | bytes 147464 | tf_op jit(solution)/shard_map/ppermute | solution.py:39
  212.7 4.2 %collective-permute-start.17 = (bf16[8,3072]{1,0:T(8,128)(2,1)S(1)}, bf16[8,3072]{1,0:T(8,128)(2,1)S(1)}, u32[]{:S(2)}, u32[]{:S(2)}) collective-permute-start(bf16[8,3072]{1,0:T(8,128)(2,1)S(1)} %get-tuple-element.11), channel_id=1, source_target_pairs={{0,0},{4,4},{8,8},{12,12},{16,16},{20,20},{24,24},{28,28},{32,32},... | collective-permute-start | bytes 147464 | tf_op jit(solution)/shard_map/ppermute | solution.py:39
  212.7 4.2 %collective-permute-start.16 = (bf16[8,3072]{1,0:T(8,128)(2,1)S(1)}, bf16[8,3072]{1,0:T(8,128)(2,1)S(1)}, u32[]{:S(2)}, u32[]{:S(2)}) collective-permute-start(bf16[8,3072]{1,0:T(8,128)(2,1)S(1)} %get-tuple-element.12), channel_id=1, source_target_pairs={{0,4},{4,8},{8,12},{12,16},{16,20},{20,24},{24,28},{28,32},{32,36}... | collective-permute-start | bytes 147464 | tf_op jit(solution)/shard_map/ppermute | solution.py:39
  245.6 39.7 %copy-start.2 = (f32[512,192]{0,1:T(8,128)S(1)}, f32[512,192]{0,1:T(8,128)}, u32[]{:S(2)}) copy-start(f32[512,192]{0,1:T(8,128)} %get-tuple-element.34) | copy-start | bytes 1179652
  261.9 16.2 %all-to-all-start.14 = ((f32[64,2,192]{2,1,0:T(2,128)}), f32[64,2,192]{2,1,0:T(2,128)S(1)}, u32[]{:S(2)}, u32[]{:S(2)}) async-start(f32[64,2,192]{2,1,0:T(2,128)} %broadcast_in_dim.88), calls=%async_computation.14 | async-start | bytes 262144 | tf_op jit(solution)/shard_map/all_to_all | solution.py:29
  (2 other events, 6.5 us)
where the time goes:
time: 288 us; the launch traced here: 286 us
  blocking collectives  104 us (36%)
  starting transfers between devices  97.3 us (34%)
  waiting for transfers between devices  41.8 us (15%)
  local copies, waits for them, and re-layouts  24.6 us (9%)
  matrix products  10.3 us (4%)
  other arithmetic  7.34 us (3%)
    ppermute x20, starting transfers between devices, passed_along(): return lax.ppermute(value, axis, pairs)  71.4 us
    all_to_all x4, blocking collectives, sent_to_all(): return lax.all_to_all(copies, axis, split_axis=0, concat_axis=0, tiled=True)  34.8 us
    all_to_all x2, blocking collectives, summed_rows(): lax.all_to_all(nearer, far, split_axis=0, concat_axis=0, tiled=True)  30.9 us
    all_to_all x4, waiting for transfers between devices, sent_to_all(): return lax.all_to_all(copies, axis, split_axis=0, concat_axis=0, tiled=True)  26.2 us
    all_to_all x2, blocking collectives, sent_and_summed(): lax.all_to_all(parts, axis, split_axis=0, concat_axis=0, tiled=True)  23.3 us
    all_to_all x4, starting transfers between devices, sent_to_all(): return lax.all_to_all(copies, axis, split_axis=0, concat_axis=0, tiled=True)  18.3 us
    all_to_all x1, blocking collectives, body(): lax.all_to_all(coeffs, 'grp', split_axis=2, concat_axis=0, tiled=True)  7.54 us
    all_to_all x1, blocking collectives, body(): lax.all_to_all(own_back.reshape(all_faces, MODES, part_rhs), 'grp', split...  7.54 us
  transfers between devices with their start and end apart: 26, of which 9 were waited for; matrix products, arithmetic and copies ran while one was open for 5% of the time, Pallas kernels for 0%

commit v1 on v0

v1 whole, which is shorter than its diff:
```python
import functools

import jax
import jax.numpy as jnp
from jax import lax
from jax.experimental import pallas as pl
from jax.experimental.pallas import tpu as pltpu
from jax.sharding import PartitionSpec as P

MORT_OWN = 16
REACH = 2
LINKS = 2 * REACH + 1
CAP = 8
NCV = 8
ITERS = 2
LANES = 128
MESH = pl.DeviceIdType.MESH
HIGHEST = lax.Precision.HIGHEST
F32 = jnp.float32
BF16 = jnp.bfloat16

relax_weight = 0.5
coarse_weight = 0.5


def iota(shape, dim):
    return lax.broadcasted_iota(jnp.int32, shape, dim)


def dot_nn(a, b):
    return lax.dot_general(a, b, (((1,), (0,)), ((), ())), preferred_element_type=F32)


def dot_nt(a, b):
    return lax.dot_general(a, b, (((1,), (1,)), ((), ())), preferred_element_type=F32)


def halves(x):
    high = x.astype(BF16)
    return high, (x - high.astype(F32)).astype(BF16)


def kernel(
    sizes,
    schur,
    rhs,
    start,
    project,
    coarse,
    owner_t,
    mortar_t,
    order_t,
    holder,
    vertex_t,
    out,
    s4,
    st,
    rh,
    tb,
    af,
    pa,
    ca,
    bd,
    sp,
    wm,
    vm,
    fac,
    acc,
    prod,
    sb,
    ar,
    zs,
    orr,
    rs,
    rr,
    ls,
    lr,
    qm,
    psc,
    dm,
    ps,
    pz,
    ks,
    kr,
    pk,
    own_tab,
    mor_tab,
    ord_tab,
    hol_tab,
    ver_tab,
    lsem,
    ag_s,
    ag_r,
    a2a_s,
    a2a_r,
    ex_s,
    ex_r,
    ret_s,
    ret_r,
    p_s,
    p_r,
    k1_s,
    k1_r,
    k2_s,
    k2_r,
    k3_s,
    k3_r,
    fin_s,
    fin_r,
):
    subs, grps, zs_n, yc_n = sizes
    s = lax.axis_index("sub")
    g = lax.axis_index("grp")
    z = s // yc_n
    yc = lax.rem(s, yc_n)
    cols = s4.shape[2]
    quarter = tb.shape[1] // grps
    half = tb.shape[1] // 2

    def sub_at(step):
        return lax.rem(s + step + subs, subs)

    def grp_at(step):
        return lax.rem(g + step, grps)

    def remote(src, dst, send, recv, where):
        return pltpu.make_async_remote_copy(
            src_ref=src,
            dst_ref=dst,
            send_sem=send,
            recv_sem=recv,
            device_id=where,
            device_id_type=MESH,
        )

    loads = [
        pltpu.make_async_copy(start, st, lsem.at[0]),
        pltpu.make_async_copy(owner_t, own_tab, lsem.at[1]),
        pltpu.make_async_copy(mortar_t, mor_tab, lsem.at[2]),
        pltpu.make_async_copy(order_t, ord_tab, lsem.at[3]),
        pltpu.make_async_copy(holder, hol_tab, lsem.at[4]),
        pltpu.make_async_copy(vertex_t, ver_tab, lsem.at[5]),
        pltpu.make_async_copy(project, pa.at[g], lsem.at[6]),
        pltpu.make_async_copy(coarse, ca.at[g], lsem.at[7]),
        pltpu.make_async_copy(rhs, rh, lsem.at[8]),
    ]
    for q in range(grps):
        loads.append(
            pltpu.make_async_copy(
                schur.at[:, pl.ds(q * cols, cols)], s4.at[q], lsem.at[9 + q]
            )
        )
    for load in loads:
        load.start()

    barrier = pltpu.get_barrier_semaphore()
    partners = [{"grp": grp_at(step)} for step in range(1, grps)]
    partners += [{"sub": sub_at(step)} for step in (-2, -1, 1, 2)]
    partners += [{"sub": lax.rem(z + step, zs_n) * yc_n + yc} for step in range(1, zs_n)]
    partners += [{"sub": z * yc_n + lax.rem(yc + step, yc_n)} for step in range(1, yc_n)]
    for where in partners:
        pl.semaphore_signal(barrier, inc=1, device_id=where, device_id_type=MESH)

    ps[...] = jnp.zeros_like(ps)
    loads[0].wait()
    tb[g] = st[...].astype(BF16)
    pl.semaphore_wait(barrier, len(partners))

    left, right = grp_at(grps - 1), grp_at(1)
    across = grp_at(2)
    top, low = pl.ds(0, half), pl.ds(half, half)

    def gather_start(buf, turn):
        to_right, to_left = {"grp": right}, {"grp": left}
        plan = [
            (buf.at[g, top], to_right),
            (buf.at[g, low], to_left),
            (buf.at[g, low], to_right),
            (buf.at[g, top], to_left),
            (buf.at[left, top], to_right),
            (buf.at[right, low], to_left),
        ]
        copies = [
            remote(ref, ref, ag_s.at[turn, i], ag_r.at[turn, i], where)
            for i, (ref, where) in enumerate(plan)
        ]
        for copy in copies[:4]:
            copy.start()
        return copies

    def gather_forward(copies):
        copies[0].wait_recv()
        copies[4].start()
        copies[1].wait_recv()
        copies[5].start()

    gathered = gather_start(tb, 0)

    for load in loads[1:6]:
        load.wait()
    stacked = jnp.concatenate(
        [own_tab[...].astype(F32), mor_tab[...].astype(F32), ver_tab[...].astype(F32)], axis=0
    ).astype(BF16)
    placed = jnp.where(
        iota((subs, subs), 0) == jnp.broadcast_to(hol_tab[...], (subs, subs)), 1.0, 0.0
    ).astype(BF16)
    moved = dot_nn(stacked, placed)
    faces = own_tab.shape[0]
    held_all, mortar_all = moved[:faces], moved[faces : 2 * faces]
    vertex_all = moved[2 * faces :]

    def column(table, index):
        mask = iota(table.shape, 1) == index
        return jnp.sum(jnp.where(mask, table, 0.0), axis=1, keepdims=True)

    square_i, square_j = iota((faces, faces), 0), iota((faces, faces), 1)

    def as_row(col):
        return jnp.sum(jnp.where(square_i == square_j, col, 0.0), axis=0, keepdims=True)

    held_c = column(held_all, s)
    held_r = as_row(held_c)
    rank_r = jnp.sum(
        jnp.where((held_c == held_r) & (square_i < square_j), 1.0, 0.0), axis=0, keepdims=True
    )
    slot_r = held_r * CAP + rank_r
    rows = iota((wm.shape[0], faces), 0)
    face_of = jnp.left_shift(jnp.right_shift(rows, 7), 3) | (rows & 7)
    slot_c = jnp.sum(
        jnp.where(iota(rows.shape, 1) == face_of, slot_r, 0.0), axis=1, keepdims=True
    )
    r_i, c_i = iota(wm.shape, 0), iota(wm.shape, 1)
    same = (jnp.right_shift(r_i, 3) & 15) == (jnp.right_shift(c_i, 3) & 15)
    slot_of = (jnp.left_shift(jnp.right_shift(c_i, 7), 3) | (c_i & 7)).astype(F32)
    wm[...] = jnp.where(same & (slot_c == slot_of), 1.0, 0.0).astype(BF16)

    width = vm.shape[1]
    lane8 = iota((faces, CAP), 1).astype(F32)
    pick8 = iota((LANES, CAP), 1) == (iota((LANES, CAP), 0) & 7)
    v_r, v_c = iota((LANES, width), 0), iota((LANES, width), 1)
    v_same = jnp.right_shift(v_r, 3) == jnp.right_shift(v_c, 4)
    v_key = (v_c & 15).astype(F32)
    counts = jnp.zeros((1, width), F32)
    for link in range(LINKS):
        sender = sub_at(REACH - link)
        hc, mc = column(held_all, sender), column(mortar_all, sender)
        hr = as_row(hc)
        rank_c = jnp.sum(
            jnp.where((hr == hc) & (square_j < square_i), 1.0, 0.0), axis=1, keepdims=True
        )
        key8 = (
            jnp.sum(
                jnp.where((hc == float(link)) & (rank_c == lane8), mc + 1.0, 0.0),
                axis=0,
                keepdims=True,
            )
            - 1.0
        )
        key_c = jnp.sum(jnp.where(pick8, key8, 0.0), axis=1, keepdims=True)
        block = jnp.where(v_same & (key_c == v_key), 1.0, 0.0)
        counts = counts + jnp.sum(block, axis=0, keepdims=True)
        vm[pl.ds(link * LANES, LANES), :] = block.astype(BF16)
    order_c = column(ord_tab[...].astype(F32), s)
    order_r = jnp.sum(
        jnp.where(iota((MORT_OWN, width), 0) == (iota((MORT_OWN, width), 1) & 15), order_c, 0.0),
        axis=0,
        keepdims=True,
    )
    inverse = 1.0 / jnp.maximum(counts, 1.0)
    row_c = iota((1, width), 1)
    for mg in range(4):
        first = (2 * mg + jnp.right_shift(row_c, 7)).astype(F32)
        second = (jnp.right_shift(row_c, 4) & 7).astype(F32)
        keep = (first <= order_r) & (second <= order_r)
        fac[pl.ds(mg, 1), :] = jnp.where(keep, inverse, 0.0)

    vertex_b = vertex_all.astype(BF16)
    d_rows, d_cols = dm.shape
    here = jnp.where(
        iota((d_rows, subs), 1) == z * yc_n + jnp.right_shift(iota((d_rows, subs), 0), 3), 1.0, 0.0
    ).astype(BF16)
    wanted = dot_nt(here, vertex_b)
    wanted = jnp.sum(
        jnp.where(iota((d_rows, NCV), 1) == (iota((d_rows, NCV), 0) & 7), wanted, 0.0),
        axis=1,
        keepdims=True,
    )
    there = jnp.where(
        iota((subs, d_cols), 0) == jnp.right_shift(iota((subs, d_cols), 1), 3) * yc_n + yc, 1.0, 0.0
    ).astype(BF16)
    given = dot_nn(vertex_b, there)
    given = jnp.sum(
        jnp.where(iota((NCV, d_cols), 0) == (iota((NCV, d_cols), 1) & 7), given, 0.0),
        axis=0,
        keepdims=True,
    )
    dm[...] = jnp.where(wanted == given, 1.0, 0.0).astype(BF16)

    lane = iota((CAP, LANES), 1)
    row8 = iota((CAP, 4 * LANES), 0)
    own_face = row8 == jnp.right_shift(iota((CAP, 4 * LANES), 1), 6)

    def build_block(q):
        def step(i, carry):
            pair = pa[q, :, pl.ds(pl.multiple_of(i * LANES, LANES), LANES)].astype(F32)
            turned = pltpu.roll(pair, LANES // 2, 1)
            even = jnp.where(lane < LANES // 2, pair, turned)
            odd = jnp.where(lane < LANES // 2, turned, pair)
            even = jnp.where(own_face, jnp.concatenate([even] * 4, axis=1), 0.0)
            odd = jnp.where(own_face, jnp.concatenate([odd] * 4, axis=1), 0.0)
            both = jnp.concatenate([even, odd], axis=0).astype(BF16)
            bd[q, pl.ds(pl.multiple_of(i * 16, 16), 16), :] = both
            return carry

        lax.fori_loop(0, pa.shape[2] // LANES, step, 0, unroll=4)

    def fold_block(q, s_block):
        wide = dot_nt(s_block, bd[q]).astype(BF16)
        for mg in range(4):
            sp[mg, :, pl.ds(pl.multiple_of(q * LANES, LANES), LANES)] = wide[
                :, mg * LANES : (mg + 1) * LANES
            ]

    def fold_coarse(q):
        basis = dot_nt(ca[q], bd[q])
        high, rest = halves(basis)
        both = jnp.concatenate([high, rest], axis=0)
        for mg in range(4):
            qm[mg, :, pl.ds(pl.multiple_of(q * LANES, LANES), LANES)] = both[
                :, mg * LANES : (mg + 1) * LANES
            ]

    loads[6].wait()
    loads[7].wait()
    build_block(g)
    for load in loads[8:]:
        load.wait()
    gather_forward(gathered)

    def add_block(q):
        acc[...] += dot_nt(tb[q], s4[q])

    acc[...] = dot_nt(tb[g], s4[g])
    gathered[2].wait_recv()
    add_block(left)
    gathered[3].wait_recv()
    add_block(right)
    gathered[4].wait_recv()
    gathered[5].wait_recv()
    add_block(across)
    prod[...] = acc[...] - rh[...]

    extra = []
    sent = list(gathered)

    def exchange(turn, residual, picked):
        coeffs = dot_nt(residual.astype(BF16), bd[g]).astype(BF16)
        for q in range(grps):
            for mg in range(4):
                sb[turn, q, pl.ds(mg * quarter, quarter), :] = coeffs[
                    q * quarter : (q + 1) * quarter, mg * LANES : (mg + 1) * LANES
                ]
        swaps = []
        for i in range(grps - 1):
            to = grp_at(i + 1)
            swap = remote(
                sb.at[turn, to], ar.at[turn, g], a2a_s.at[turn, i], a2a_r.at[turn, i], {"grp": to}
            )
            swap.start()
            swaps.append(swap)
        ar[turn, g] = sb[turn, g]
        if turn == 0:
            for i in range(grps - 1):
                to = grp_at(i + 1)
                extra.append(remote(ca.at[g], ca.at[g], p_s.at[0, i], p_r.at[0, i], {"grp": to}))
                extra.append(remote(pa.at[g], pa.at[g], p_s.at[1, i], p_r.at[1, i], {"grp": to}))
            for copy in extra:
                copy.start()
            fold_block(g, s4[g])
            fold_coarse(g)
        for swap in swaps:
            swap.wait_recv()
        lines = [ar[turn, q] for q in range(grps)]
        if picked is not None:
            narrow = picked()
            for q in range(grps):
                term = jnp.dot(
                    narrow, psc[q], preferred_element_type=F32, precision=HIGHEST
                )
                tall = jnp.concatenate(
                    [term[:, mg * LANES : (mg + 1) * LANES] for mg in range(4)], axis=0
                )
                lines[q] = (lines[q].astype(F32) - coarse_weight * tall).astype(BF16)
        grouped = dot_nn(jnp.concatenate(lines, axis=1), wm[...]).astype(BF16)
        sends = []
        for link in (0, 4, 1, 3, 2):
            part = grouped[:, link * LANES : (link + 1) * LANES]
            if link == REACH:
                orr[turn, link] = part
                continue
            zs[turn, link] = part
            copy = remote(
                zs.at[turn, link],
                orr.at[turn, link],
                ex_s.at[turn, link],
                ex_r.at[turn, link],
                {"sub": sub_at(link - REACH)},
            )
            copy.start()
            sends.append(copy)
        if turn == 0:
            for copy in extra:
                copy.wait_recv()
            for i in range(grps - 1):
                build_block(grp_at(i + 1))
        for copy in sends:
            copy.wait_recv()
        joined = jnp.concatenate([orr[turn, link] for link in range(LINKS)], axis=1)
        sums = dot_nn(joined, vm[...])
        averages = jnp.concatenate(
            [
                sums[mg * quarter : (mg + 1) * quarter] * fac[pl.ds(mg, 1), :]
                for mg in range(4)
            ],
            axis=0,
        ).astype(BF16)
        replies = dot_nt(averages, vm[...]).astype(BF16)
        backs = []
        for link in (0, 4, 1, 3, 2):
            part = replies[:, link * LANES : (link + 1) * LANES]
            if link == REACH:
                rr[turn, link] = part
                continue
            rs[turn, link] = part
            copy = remote(
                rs.at[turn, link],
                rr.at[turn, link],
                ret_s.at[turn, link],
                ret_r.at[turn, link],
                {"sub": sub_at(REACH - link)},
            )
            copy.start()
            backs.append(copy)
        if turn == 0:
            for i in range(grps - 1):
                q = grp_at(i + 1)
                fold_block(q, s4[q])
                fold_coarse(q)
            spread = dot_nt(ca[0], s4[0])
            for q in range(1, grps):
                spread = spread + dot_nt(ca[q], s4[q])
            high, rest = halves(spread)
            psc[g] = dot_nt(high, bd[g]) + dot_nt(rest, bd[g])
            for i in range(grps - 1):
                to = grp_at(i + 1)
                copy = remote(psc.at[g], psc.at[g], p_s.at[2, i], p_r.at[2, i], {"grp": to})
                copy.start()
                extra.append(copy)
        for copy in backs:
            copy.wait_recv()
        sent.extend(swaps + sends + backs)
        answered = jnp.concatenate([rr[turn, link] for link in range(LINKS)], axis=1)
        return dot_nt(answered, wm[...]).astype(BF16)

    def coarse_first(turn, mine):
        value = dot_nt(qm[0], mine[:quarter])
        for mg in range(1, 4):
            value = value + dot_nt(qm[mg], mine[mg * quarter : (mg + 1) * quarter])
        ps[turn, :, pl.ds(0, quarter)] = value[:NCV] + value[NCV:]
        copies = []
        for i in range(zs_n - 1):
            to = lax.rem(z + i + 1, zs_n) * yc_n + yc
            copy = remote(
                ps.at[turn], pz.at[turn, z], k1_s.at[turn, i], k1_r.at[turn, i], {"sub": to}
            )
            copy.start()
            copies.append(copy)
        pz[turn, z] = ps[turn]
        sent.extend(copies)
        return copies

    def coarse_second(turn, copies):
        for copy in copies:
            copy.wait_recv()
        high, rest = halves(pz[turn].reshape(zs_n * NCV, LANES))
        value = dot_nn(dm[...], high) + dot_nn(dm[...], rest)
        ks[turn] = value.reshape(yc_n, NCV, LANES)
        copies = []
        for i in range(yc_n - 1):
            to = lax.rem(yc + i + 1, yc_n)
            copy = remote(
                ks.at[turn, to],
                kr.at[turn, yc],
                k2_s.at[turn, i],
                k2_r.at[turn, i],
                {"sub": z * yc_n + to},
            )
            copy.start()
            copies.append(copy)
        kr[turn, yc] = ks[turn, yc]
        sent.extend(copies)
        return copies

    mine = exchange(0, prod[...], None)
    af[g] = mine
    gathered = gather_start(af, 1)
    sent.extend(gathered)
    first_copies = coarse_first(0, mine)

    def add_modes(q):
        value = dot_nt(af[q, pl.ds(0, quarter), :], sp[0])
        for mg in range(1, 4):
            value = value + dot_nt(af[q, pl.ds(mg * quarter, quarter), :], sp[mg])
        at = pl.ds(pl.multiple_of(q * quarter, quarter), quarter)
        acc[at, :] = prod[at, :] - relax_weight * value

    add_modes(g)
    gather_forward(gathered)
    gathered[2].wait_recv()
    add_modes(left)
    gathered[3].wait_recv()
    add_modes(right)
    second_copies = coarse_second(0, first_copies)
    gathered[4].wait_recv()
    gathered[5].wait_recv()
    add_modes(across)
    for copy in extra[2 * (grps - 1) :]:
        copy.wait_recv()
    totals = []

    def first_picked():
        for copy in second_copies:
            copy.wait_recv()
        picked = jnp.sum(kr[0], axis=0)
        totals.append(picked)
        return picked.T[:quarter]

    mine = exchange(1, acc[...], first_picked)
    first_copies = coarse_first(1, mine)
    backs = []
    for q in range(grps):
        ls[q] = mine[:, q * LANES : (q + 1) * LANES]
    for i in range(grps - 1):
        to = grp_at(i + 1)
        copy = remote(ls.at[to], lr.at[g], fin_s.at[i], fin_r.at[i], {"grp": to})
        copy.start()
        backs.append(copy)
    lr[g] = ls[g]

    def own_rows(blocks):
        lines = [
            jnp.concatenate(
                [block[mg * quarter : (mg + 1) * quarter] for mg in range(4)], axis=1
            )
            for block in blocks
        ]
        return jnp.concatenate(lines, axis=0)

    here = pl.ds(pl.multiple_of(g * LANES, LANES), LANES)
    lifted = dot_nn(own_rows([af[q, :, here] for q in range(grps)]), bd[g])
    for copy in backs:
        copy.wait_recv()
    lifted = lifted + dot_nn(own_rows([lr[q] for q in range(grps)]), bd[g])
    acc[...] = st[...] - relax_weight * lifted

    second_copies = coarse_second(1, first_copies)
    for copy in second_copies:
        copy.wait_recv()
    pk[g] = jnp.sum(kr[1], axis=0) + totals[0]
    last = []
    for i in range(grps - 1):
        to = grp_at(i + 1)
        copy = remote(pk.at[g], pk.at[g], k3_s.at[i], k3_r.at[i], {"grp": to})
        copy.start()
        last.append(copy)
    for copy in last:
        copy.wait_recv()
    tall = jnp.concatenate([pk[q].T[:quarter] for q in range(grps)], axis=0)
    corr = jnp.dot(
        tall, ca[g].astype(F32), preferred_element_type=F32, precision=HIGHEST
    )
    out[...] = acc[...] - coarse_weight * corr
    for copy in sent + extra + backs + last:
        copy.wait_send()


def solution(mesh):
    subs, grps = mesh.shape["sub"], mesh.shape["grp"]
    zs_n = 8 if subs == 128 else 2
    yc_n = subs // zs_n
    sizes = (subs, grps, zs_n, yc_n)

    def body(
        schur,
        rhs,
        start,
        project,
        coarse_basis,
        owner_of_face,
        mortar_of_face,
        mortar_order,
        subdomain_map,
        vertex_ids,
    ):
        rows, cols = schur.shape[1], schur.shape[2]
        part = cols // grps
        wide = rhs.shape[2]
        faces = owner_of_face.shape[1]
        block = LANES
        dma = pltpu.SemaphoreType.DMA
        vmem = pltpu.VMEM
        scratch = [
            vmem((grps, rows, part), BF16),
            vmem((wide, rows), F32),
            vmem((wide, rows), F32),
            vmem((grps, wide, rows), BF16),
            vmem((grps, wide, rows), BF16),
            vmem((grps,) + project.shape[1:], BF16),
            vmem((grps,) + coarse_basis.shape[1:], BF16),
            vmem((grps, rows, rows), BF16),
            vmem((4, rows, rows), BF16),
            vmem((rows, LINKS * block), BF16),
            vmem((LINKS * block, 16 * MORT_OWN), BF16),
            vmem((8, 16 * MORT_OWN), F32),
            vmem((wide, rows), F32),
            vmem((wide, rows), F32),
            vmem((ITERS, grps, wide, block), BF16),
            vmem((ITERS, grps, wide, block), BF16),
            vmem((ITERS, LINKS, wide, block), BF16),
            vmem((ITERS, LINKS, wide, block), BF16),
            vmem((ITERS, LINKS, wide, block), BF16),
            vmem((ITERS, LINKS, wide, block), BF16),
            vmem((grps, wide, block), BF16),
            vmem((grps, wide, block), BF16),
            vmem((4, 2 * NCV, rows), BF16),
            vmem((grps, NCV, rows), F32),
            vmem((yc_n * NCV, zs_n * NCV), BF16),
            vmem((ITERS, NCV, LANES), F32),
            vmem((ITERS, zs_n, NCV, LANES), F32),
            vmem((ITERS, yc_n, NCV, LANES), F32),
            vmem((ITERS, yc_n, NCV, LANES), F32),
            vmem((grps, NCV, LANES), F32),
            vmem((faces, subs), jnp.int32),
            vmem((faces, subs), jnp.int32),
            vmem((MORT_OWN, subs), jnp.int32),
            vmem((1, subs), jnp.int32),
            vmem((NCV, subs), jnp.int32),
            dma((9 + grps,)),
            dma((2, 6)),
            dma((2, 6)),
            dma((ITERS, grps - 1)),
            dma((ITERS, grps - 1)),
            dma((ITERS, LINKS)),
            dma((ITERS, LINKS)),
            dma((ITERS, LINKS)),
            dma((ITERS, LINKS)),
            dma((3, grps - 1)),
            dma((3, grps - 1)),
            dma((ITERS, zs_n - 1)),
            dma((ITERS, zs_n - 1)),
            dma((ITERS, yc_n - 1)),
            dma((ITERS, yc_n - 1)),
            dma((grps - 1,)),
            dma((grps - 1,)),
            dma((grps - 1,)),
            dma((grps - 1,)),
        ]
        result = pl.pallas_call(
            functools.partial(kernel, sizes),
            out_shape=jax.ShapeDtypeStruct((wide, rows), F32),
            in_specs=[pl.BlockSpec(memory_space=pltpu.HBM)] * 10,
            out_specs=pl.BlockSpec(memory_space=pltpu.VMEM),
            scratch_shapes=scratch,
            compiler_params=pltpu.CompilerParams(
                collective_id=0, has_side_effects=True, vmem_limit_bytes=66 * 1000 * 1000
            ),
        )(
            schur[0],
            rhs[0].T,
            start[0].T,
            project[0],
            coarse_basis[0],
            owner_of_face[:, :, 0].T,
            mortar_of_face.T,
            mortar_order.T,
            subdomain_map.reshape(1, subs),
            vertex_ids.T,
        )
        return result.T[None]

    split = P("sub", "grp", None)
    return jax.shard_map(
        body,
        mesh=mesh,
        in_specs=(split, split, split, split, P("sub", None, "grp"), P(), P(), P(), P(), P()),
        out_specs=split,
        check_vma=False,
    )
```

time: 288 us -> 82.6 us (0.29)
  blocking collectives: 104 us -> 0 us
  starting transfers between devices: 97.3 us -> 0 us
  Pallas kernels: 0 us -> 80 us
  waiting for transfers between devices: 41.8 us -> 0 us
  local copies, waits for them, and re-layouts: 24.6 us -> 1.77 us
  matrix products: 10.3 us -> 0 us
  other arithmetic: 7.34 us -> 0 us
    all_to_all x10 -> x0, blocking collectives: 104 us -> none  [the longest x4 34.8 us: sent_to_all(): return lax.all_to_all(copies, axis, split_axis=0, concat_axis=0, tiled=True)]
    pallas_call x0 -> x1, Pallas kernels: none -> 80 us  [body(): pl.pallas_call(functools.partial(kernel, sizes), out_shape=jax.ShapeDtype...]
    ppermute x20 -> x0, starting transfers between devices: 71.4 us -> none  [passed_along(): return lax.ppermute(value, axis, pairs)]
    all_to_all x6 -> x0, waiting for transfers between devices: 34.9 us -> none  [the longest x4 26.2 us: sent_to_all(): return lax.all_to_all(copies, axis, split_axis=0, concat_axis=0, tiled=True)]
    all_to_all x6 -> x0, starting transfers between devices: 25.9 us -> none  [the longest x4 18.3 us: sent_to_all(): return lax.all_to_all(copies, axis, split_axis=0, concat_axis=0, tiled=True)]
    dot_general x24 -> x0, matrix products: 10.3 us -> none  [the longest x2 2.35 us: body(): lax.dot_general(coarse_wide, picked, contract_first, precision=highest)]
    ppermute x20 -> x0, waiting for transfers between devices: 6.89 us -> none  [passed_along(): return lax.ppermute(value, axis, pairs)]
    gather x6 -> x0, local copies, waits for them, and re-layouts: 4.7 us -> none  [the longest x1 1.39 us: body(): from_mortar = jnp.take(mortar_local, senders, axis=0)]
  transfers between devices with their start and end apart: 26 -> 0, of which waited for: 9 -> 0; matrix products, arithmetic and copies ran while one was open for 5% -> 0% of each run, Pallas kernels for 0% -> 0%
where the time goes in v1:
time: 82.6 us; the launch traced here: 81.8 us
  Pallas kernels  80 us (97%)
  local copies, waits for them, and re-layouts  1.77 us (2%)
    pallas_call x1, Pallas kernels, body(): pl.pallas_call(functools.partial(kernel, sizes), out_shape=jax.ShapeDtype...  80 us
    unnamed x1, local copies, waits for them, and re-layouts  1.77 us

profile of v1, /device:TPU:1, one launch (start us, length us, event | category | flops | bytes accessed | tf_op | source)
XLA Modules:
  0.0 81.8 jit_solution(10012030657474983052)
XLA Ops:
  0.0 80.0 %shard_map.100 = f32[192,512]{1,0:T(8,128)} custom-call(bf16[512,2048]{1,0:T(8,128)(2,1)} %bitcast.19, f32[192,512]{1,0:T(8,128)} %bitcast.21, f32[192,512]{1,0:T(8,128)} %bitcast.22, bf16[8,4096]{1,0:T(8,128)(2,1)} %bitcast.23, bf16[8,512]{1,0:T(8,128)(2,1)} %bitcast.26, s32[32,128]{1,0:T(8,128)} %bitcast.24, s32[32,128]{1,0:T(8,128)} %bitcast.25, ...), custom_call_target="tpu_custom_call" | custom-call | tf_op jit(solution)/shard_map/pallas_call | solution.py:668
  80.0 1.8 %copy.12 = f32[1,512,192]{1,2,0:T(8,128)} copy(f32[1,512,192]{1,2,0:T(8,128)} %bitcast.20) | data formatting | bytes 786432

commit v2 on v1

v2 whole, which is shorter than its diff:
```python
import functools

import jax
import jax.numpy as jnp
from jax import lax
from jax.experimental import pallas as pl
from jax.experimental.pallas import tpu as pltpu
from jax.sharding import PartitionSpec as P

MORT_OWN = 16
REACH = 2
LINKS = 2 * REACH + 1
CAP = 8
NCV = 8
ITERS = 2
PARTS = 2
LANES = 128
MESH = pl.DeviceIdType.MESH
HIGHEST = lax.Precision.HIGHEST
F32 = jnp.float32
BF16 = jnp.bfloat16

relax_weight = 0.5
coarse_weight = 0.5


def iota(shape, dim):
    return lax.broadcasted_iota(jnp.int32, shape, dim)


def dot_nn(a, b):
    return lax.dot_general(a, b, (((1,), (0,)), ((), ())), preferred_element_type=F32)


def dot_nt(a, b):
    return lax.dot_general(a, b, (((1,), (1,)), ((), ())), preferred_element_type=F32)


def halves(x):
    high = x.astype(BF16)
    return high, (x - high.astype(F32)).astype(BF16)


def kernel(
    sizes,
    schur,
    rhs,
    start,
    project,
    coarse,
    owner_t,
    mortar_t,
    order_t,
    holder,
    vertex_t,
    out,
    s4,
    st,
    rh,
    tb,
    af,
    pa,
    ca,
    bd,
    sp,
    wm,
    vm,
    fac,
    acc,
    prod,
    sb,
    ar,
    zs,
    orr,
    rs,
    rr,
    ls,
    lr,
    qm,
    psc,
    dm,
    ps,
    pz,
    ks,
    kr,
    pk,
    own_tab,
    mor_tab,
    ord_tab,
    hol_tab,
    ver_tab,
    lsem,
    ag_s,
    ag_r,
    a2a_s,
    a2a_r,
    ex_s,
    ex_r,
    ret_s,
    ret_r,
    p_s,
    p_r,
    k1_s,
    k1_r,
    k2_s,
    k2_r,
    k3_s,
    k3_r,
    fin_s,
    fin_r,
):
    subs, grps, zs_n, yc_n = sizes
    s = lax.axis_index("sub")
    g = lax.axis_index("grp")
    z = s // yc_n
    yc = lax.rem(s, yc_n)
    cols = s4.shape[2]
    quarter = tb.shape[1] // grps
    half = tb.shape[1] // 2

    def sub_at(step):
        return lax.rem(s + step + subs, subs)

    def grp_at(step):
        return lax.rem(g + step, grps)

    def remote(src, dst, send, recv, where):
        return pltpu.make_async_remote_copy(
            src_ref=src,
            dst_ref=dst,
            send_sem=send,
            recv_sem=recv,
            device_id=where,
            device_id_type=MESH,
        )

    def whole(ref, sem):
        return remote(ref, ref, sem, sem, {"grp": grp_at(1)})

    def arrive(name, *parts):
        with jax.named_scope(name):
            for ref, sem in parts:
                whole(ref, sem).wait_recv()

    barrier = pltpu.get_barrier_semaphore()
    partners = [{"sub": lax.rem(z + step, zs_n) * yc_n + yc} for step in range(1, zs_n)]
    partners += [{"sub": z * yc_n + lax.rem(yc + step, yc_n)} for step in range(1, yc_n)]
    partners += [{"sub": sub_at(step)} for step in (-2, -1, 1, 2)]
    partners += [{"grp": grp_at(step)} for step in range(1, grps)]
    for where in partners:
        pl.semaphore_signal(barrier, inc=1, device_id=where, device_id_type=MESH)

    loads = [
        pltpu.make_async_copy(start, st, lsem.at[0]),
        pltpu.make_async_copy(owner_t, own_tab, lsem.at[1]),
        pltpu.make_async_copy(mortar_t, mor_tab, lsem.at[2]),
        pltpu.make_async_copy(order_t, ord_tab, lsem.at[3]),
        pltpu.make_async_copy(holder, hol_tab, lsem.at[4]),
        pltpu.make_async_copy(vertex_t, ver_tab, lsem.at[5]),
        pltpu.make_async_copy(project, pa.at[g], lsem.at[6]),
        pltpu.make_async_copy(coarse, ca.at[g], lsem.at[7]),
        pltpu.make_async_copy(rhs, rh, lsem.at[8]),
    ]
    for q in range(grps):
        loads.append(
            pltpu.make_async_copy(
                schur.at[:, pl.ds(q * cols, cols)], s4.at[q], lsem.at[9 + q]
            )
        )
    for load in loads:
        load.start()

    with jax.named_scope("w_start"):
        loads[0].wait()
    tb[g] = st[...].astype(BF16)
    with jax.named_scope("w_barrier"):
        pl.semaphore_wait(barrier, len(partners))

    left, right = grp_at(grps - 1), grp_at(1)
    across = grp_at(2)
    to_right, to_left = {"grp": right}, {"grp": left}

    def gather_plan(buf, turn):
        def piece(q, i):
            return buf.at[q, pl.ds(i * quarter, quarter)]

        def send(q, i, place, where):
            ref = piece(q, i)
            remote(ref, ref, ag_s.at[turn], ag_r.at[turn, place], where).start()

        far = [2 * grps + turn * (i // 2) for i in range(grps)]
        return piece, send, far

    def gather_send(plan, i):
        _, send, _ = plan
        send(g, i, i, to_right)
        send(g, i + 1, grps + i + 1, to_left)
        send(g, i + 1, i + 1, to_right)
        send(g, i, grps + i, to_left)

    def from_left(plan, turn, i):
        return plan[0](left, i), ag_r.at[turn, i]

    def from_right(plan, turn, i):
        return plan[0](right, i), ag_r.at[turn, grps + i]

    def gather_forward(plan, turn, i):
        _, send, far = plan
        if i % 2:
            arrive("w_near", from_right(plan, turn, i))
            send(right, i, far[i], to_left)
        else:
            arrive("w_near", from_left(plan, turn, i))
            send(left, i, far[i], to_right)

    gathered = gather_plan(tb, 0)
    for i in range(0, grps, 2):
        gather_send(gathered, i)

    ps[...] = jnp.zeros_like(ps)
    for load in loads[1:6]:
        load.wait()
    stacked = jnp.concatenate(
        [own_tab[...].astype(F32), mor_tab[...].astype(F32), ver_tab[...].astype(F32)], axis=0
    ).astype(BF16)
    placed = jnp.where(
        iota((subs, subs), 0) == jnp.broadcast_to(hol_tab[...], (subs, subs)), 1.0, 0.0
    ).astype(BF16)
    moved = dot_nn(stacked, placed)
    faces = own_tab.shape[0]
    held_all, mortar_all = moved[:faces], moved[faces : 2 * faces]
    vertex_all = moved[2 * faces :]

    def column(table, index):
        mask = iota(table.shape, 1) == index
        return jnp.sum(jnp.where(mask, table, 0.0), axis=1, keepdims=True)

    square_i, square_j = iota((faces, faces), 0), iota((faces, faces), 1)

    def as_row(col):
        return jnp.sum(jnp.where(square_i == square_j, col, 0.0), axis=0, keepdims=True)

    held_c = column(held_all, s)
    held_r = as_row(held_c)
    rank_r = jnp.sum(
        jnp.where((held_c == held_r) & (square_i < square_j), 1.0, 0.0), axis=0, keepdims=True
    )
    slot_r = held_r * CAP + rank_r
    rows = iota((wm.shape[0], faces), 0)
    face_of = jnp.left_shift(jnp.right_shift(rows, 7), 3) | (rows & 7)
    slot_c = jnp.sum(
        jnp.where(iota(rows.shape, 1) == face_of, slot_r, 0.0), axis=1, keepdims=True
    )
    r_i, c_i = iota(wm.shape, 0), iota(wm.shape, 1)
    same = (jnp.right_shift(r_i, 3) & 15) == (jnp.right_shift(c_i, 3) & 15)
    slot_of = (jnp.left_shift(jnp.right_shift(c_i, 7), 3) | (c_i & 7)).astype(F32)
    wm[...] = jnp.where(same & (slot_c == slot_of), 1.0, 0.0).astype(BF16)

    width = vm.shape[1]
    lane8 = iota((faces, CAP), 1).astype(F32)
    pick8 = iota((LANES, CAP), 1) == (iota((LANES, CAP), 0) & 7)
    v_r, v_c = iota((LANES, width), 0), iota((LANES, width), 1)
    v_same = jnp.right_shift(v_r, 3) == jnp.right_shift(v_c, 4)
    v_key = (v_c & 15).astype(F32)
    counts = jnp.zeros((1, width), F32)
    for link in range(LINKS):
        sender = sub_at(REACH - link)
        hc, mc = column(held_all, sender), column(mortar_all, sender)
        hr = as_row(hc)
        rank_c = jnp.sum(
            jnp.where((hr == hc) & (square_j < square_i), 1.0, 0.0), axis=1, keepdims=True
        )
        key8 = (
            jnp.sum(
                jnp.where((hc == float(link)) & (rank_c == lane8), mc + 1.0, 0.0),
                axis=0,
                keepdims=True,
            )
            - 1.0
        )
        key_c = jnp.sum(jnp.where(pick8, key8, 0.0), axis=1, keepdims=True)
        block = jnp.where(v_same & (key_c == v_key), 1.0, 0.0)
        counts = counts + jnp.sum(block, axis=0, keepdims=True)
        vm[pl.ds(link * LANES, LANES), :] = block.astype(BF16)
    order_c = column(ord_tab[...].astype(F32), s)
    order_r = jnp.sum(
        jnp.where(iota((MORT_OWN, width), 0) == (iota((MORT_OWN, width), 1) & 15), order_c, 0.0),
        axis=0,
        keepdims=True,
    )
    inverse = 1.0 / jnp.maximum(counts, 1.0)
    row_c = iota((1, width), 1)
    for mg in range(4):
        first = (2 * mg + jnp.right_shift(row_c, 7)).astype(F32)
        second = (jnp.right_shift(row_c, 4) & 7).astype(F32)
        keep = (first <= order_r) & (second <= order_r)
        fac[pl.ds(mg, 1), :] = jnp.where(keep, inverse, 0.0)

    vertex_b = vertex_all.astype(BF16)
    d_rows, d_cols = dm.shape
    here = jnp.where(
        iota((d_rows, subs), 1) == z * yc_n + jnp.right_shift(iota((d_rows, subs), 0), 3), 1.0, 0.0
    ).astype(BF16)
    wanted = dot_nt(here, vertex_b)
    wanted = jnp.sum(
        jnp.where(iota((d_rows, NCV), 1) == (iota((d_rows, NCV), 0) & 7), wanted, 0.0),
        axis=1,
        keepdims=True,
    )
    there = jnp.where(
        iota((subs, d_cols), 0) == jnp.right_shift(iota((subs, d_cols), 1), 3) * yc_n + yc, 1.0, 0.0
    ).astype(BF16)
    given = dot_nn(vertex_b, there)
    given = jnp.sum(
        jnp.where(iota((NCV, d_cols), 0) == (iota((NCV, d_cols), 1) & 7), given, 0.0),
        axis=0,
        keepdims=True,
    )
    dm[...] = jnp.where(wanted == given, 1.0, 0.0).astype(BF16)

    lane = iota((CAP, LANES), 1)
    row8 = iota((CAP, 4 * LANES), 0)
    own_face = row8 == jnp.right_shift(iota((CAP, 4 * LANES), 1), 6)

    def build_block(q):
        def step(i, carry):
            pair = pa[q, :, pl.ds(pl.multiple_of(i * LANES, LANES), LANES)].astype(F32)
            turned = pltpu.roll(pair, LANES // 2, 1)
            even = jnp.where(lane < LANES // 2, pair, turned)
            odd = jnp.where(lane < LANES // 2, turned, pair)
            even = jnp.where(own_face, jnp.concatenate([even] * 4, axis=1), 0.0)
            odd = jnp.where(own_face, jnp.concatenate([odd] * 4, axis=1), 0.0)
            both = jnp.concatenate([even, odd], axis=0).astype(BF16)
            bd[q, pl.ds(pl.multiple_of(i * 16, 16), 16), :] = both
            return carry

        lax.fori_loop(0, pa.shape[2] // LANES, step, 0, unroll=4)

    def fold_block(q, s_block):
        wide = dot_nt(s_block, bd[q]).astype(BF16)
        for mg in range(4):
            sp[mg, :, pl.ds(pl.multiple_of(q * LANES, LANES), LANES)] = wide[
                :, mg * LANES : (mg + 1) * LANES
            ]

    def fold_coarse(q):
        both = jnp.concatenate(halves(dot_nt(ca[q], bd[q])), axis=0)
        for mg in range(4):
            qm[mg, :, pl.ds(pl.multiple_of(q * LANES, LANES), LANES)] = both[
                :, mg * LANES : (mg + 1) * LANES
            ]

    loads[6].wait()
    loads[7].wait()
    with jax.named_scope("c_block"):
        build_block(g)
    with jax.named_scope("w_loads"):
        for load in loads[8:]:
            load.wait()
    for i in range(grps):
        gather_forward(gathered, 0, i)

    def add_block(q):
        acc[...] += dot_nt(tb[q], s4[q])

    acc[...] = dot_nt(tb[g], s4[g])
    arrive("w_left", from_left(gathered, 0, 1), from_left(gathered, 0, 3))
    add_block(left)
    arrive("w_right", from_right(gathered, 0, 0), from_right(gathered, 0, 2))
    add_block(right)
    arrive("w_across", (tb.at[across], ag_r.at[0, 2 * grps]))
    add_block(across)
    prod[...] = acc[...] - rh[...]

    groups = 4 // PARTS
    span = groups * quarter

    def rows_of(part):
        return pl.ds(part * span, span)

    def exchange(turn, residual, picked, deliver):
        residual = residual.astype(BF16)
        for part in range(PARTS):
            first = part * groups
            modes = bd[g, pl.ds(first * LANES, groups * LANES), :]
            coeffs = dot_nt(residual, modes).astype(BF16)
            for q in range(grps):
                for mg in range(groups):
                    sb[turn, q, pl.ds((first + mg) * quarter, quarter), :] = coeffs[
                        q * quarter : (q + 1) * quarter, mg * LANES : (mg + 1) * LANES
                    ]
            for i in (2, 1, 3):
                to = grp_at(i)
                remote(
                    sb.at[turn, to, rows_of(part)],
                    ar.at[turn, g, rows_of(part)],
                    a2a_s.at[turn],
                    a2a_r.at[turn, part],
                    {"grp": to},
                ).start()
        ar[turn, g] = sb[turn, g]
        if turn == 0:
            for i, ref in enumerate((ca, pa)):
                for step in (2, 1, 3):
                    where = {"grp": grp_at(step)}
                    remote(ref.at[g], ref.at[g], p_s.at[i], p_r.at[i], where).start()
            fold_block(g, s4[g])
            fold_coarse(g)
        terms = None if picked is None else picked()
        for part in range(PARTS):
            arrive("w_a2a", (ar.at[turn, pl.ds(0, grps - 1), rows_of(part)], a2a_r.at[turn, part]))
            lines = [ar[turn, q, rows_of(part), :] for q in range(grps)]
            if terms is not None:
                for q in range(grps):
                    tall = jnp.concatenate(
                        [
                            terms[q][:, mg * LANES : (mg + 1) * LANES]
                            for mg in range(part * groups, (part + 1) * groups)
                        ],
                        axis=0,
                    )
                    lines[q] = (lines[q].astype(F32) - coarse_weight * tall).astype(BF16)
            grouped = dot_nn(jnp.concatenate(lines, axis=1), wm[...]).astype(BF16)
            for link in (0, 4, 1, 3, 2):
                piece = grouped[:, link * LANES : (link + 1) * LANES]
                if link == REACH:
                    orr[turn, link, rows_of(part), :] = piece
                    continue
                zs[turn, link, rows_of(part), :] = piece
                remote(
                    zs.at[turn, link, rows_of(part)],
                    orr.at[turn, link, rows_of(part)],
                    ex_s.at[turn],
                    ex_r.at[turn, part],
                    {"sub": sub_at(link - REACH)},
                ).start()
        if turn == 0:
            others = pl.ds(0, grps - 1)
            arrive("w_extra", (ca.at[others], p_r.at[0]), (pa.at[others], p_r.at[1]))
            for i in range(grps - 1):
                build_block(grp_at(i + 1))
        for part in range(PARTS):
            arrive("w_ex", (orr.at[turn, pl.ds(0, LINKS - 1), rows_of(part)], ex_r.at[turn, part]))
            joined = jnp.concatenate(
                [orr[turn, link, rows_of(part), :] for link in range(LINKS)], axis=1
            )
            sums = dot_nn(joined, vm[...])
            averages = jnp.concatenate(
                [
                    sums[mg * quarter : (mg + 1) * quarter]
                    * fac[pl.ds(part * groups + mg, 1), :]
                    for mg in range(groups)
                ],
                axis=0,
            ).astype(BF16)
            replies = dot_nt(averages, vm[...]).astype(BF16)
            for link in (0, 4, 1, 3, 2):
                piece = replies[:, link * LANES : (link + 1) * LANES]
                if link == REACH:
                    rr[turn, link, rows_of(part), :] = piece
                    continue
                rs[turn, link, rows_of(part), :] = piece
                remote(
                    rs.at[turn, link, rows_of(part)],
                    rr.at[turn, link, rows_of(part)],
                    ret_s.at[turn],
                    ret_r.at[turn, part],
                    {"sub": sub_at(REACH - link)},
                ).start()
        if turn == 0:
            for i in range(grps - 1):
                q = grp_at(i + 1)
                fold_block(q, s4[q])
                fold_coarse(q)
            spread = dot_nt(ca[0], s4[0])
            for q in range(1, grps):
                spread = spread + dot_nt(ca[q], s4[q])
            high, rest = halves(spread)
            psc[g] = jnp.concatenate(
                halves(dot_nt(high, bd[g]) + dot_nt(rest, bd[g])), axis=0
            )
            for step in (2, 1, 3):
                where = {"grp": grp_at(step)}
                remote(psc.at[g], psc.at[g], p_s.at[2], p_r.at[2], where).start()
        for part in range(PARTS):
            arrive("w_ret", (rr.at[turn, pl.ds(0, LINKS - 1), rows_of(part)], ret_r.at[turn, part]))
            answered = jnp.concatenate(
                [rr[turn, link, rows_of(part), :] for link in range(LINKS)], axis=1
            )
            deliver(part, dot_nt(answered, wm[...]).astype(BF16))

    def coarse_part(part, mine):
        value = dot_nt(qm[part * groups], mine[:quarter])
        for mg in range(1, groups):
            value = value + dot_nt(
                qm[part * groups + mg], mine[mg * quarter : (mg + 1) * quarter]
            )
        return value[:NCV] + value[NCV:]

    def coarse_first(turn, value):
        ps[turn, :, pl.ds(0, quarter)] = value
        for step in range(zs_n - 1):
            to = lax.rem(z + step + 1, zs_n) * yc_n + yc
            remote(
                ps.at[turn], pz.at[turn, z], k1_s.at[turn], k1_r.at[turn], {"sub": to}
            ).start()
        pz[turn, z] = ps[turn]

    def coarse_second(turn):
        arrive("w_k1", (pz.at[turn, pl.ds(0, zs_n - 1)], k1_r.at[turn]))
        high, rest = halves(pz[turn].reshape(zs_n * NCV, LANES))
        value = dot_nn(dm[...], high) + dot_nn(dm[...], rest)
        ks[turn] = value.reshape(yc_n, NCV, LANES)
        for step in range(yc_n - 1):
            to = lax.rem(yc + step + 1, yc_n)
            remote(
                ks.at[turn, to],
                kr.at[turn, yc],
                k2_s.at[turn],
                k2_r.at[turn],
                {"sub": z * yc_n + to},
            ).start()
        kr[turn, yc] = ks[turn, yc]

    def coarse_third(turn):
        arrive("w_k2", (kr.at[turn, pl.ds(0, yc_n - 1)], k2_r.at[turn]))
        return jnp.sum(kr[turn], axis=0)

    gathered = gather_plan(af, 1)
    sums = []

    def spread_out(part, mine):
        af[g, rows_of(part), :] = mine
        for i in range(part * groups, (part + 1) * groups, 2):
            gather_send(gathered, i)
        sums.append(coarse_part(part, mine))
        if part == PARTS - 1:
            coarse_first(0, sum(sums))

    exchange(0, prod[...], None, spread_out)

    def add_modes(q, groups_of, fresh):
        at = pl.ds(pl.multiple_of(q * quarter, quarter), quarter)
        value = dot_nt(af[q, pl.ds(groups_of[0] * quarter, quarter), :], sp[groups_of[0]])
        for mg in groups_of[1:]:
            value = value + dot_nt(af[q, pl.ds(mg * quarter, quarter), :], sp[mg])
        base = prod if fresh else acc
        acc[at, :] = base[at, :] - relax_weight * value

    add_modes(g, (0, 1, 2, 3), True)
    gather_forward(gathered, 1, 0)
    gather_forward(gathered, 1, 1)
    arrive("w_left", from_left(gathered, 1, 1))
    add_modes(left, (0, 1), True)
    arrive("w_right", from_right(gathered, 1, 0))
    add_modes(right, (0, 1), True)
    gather_forward(gathered, 1, 2)
    gather_forward(gathered, 1, 3)
    coarse_second(0)
    arrive("w_left", from_left(gathered, 1, 3))
    add_modes(left, (2, 3), False)
    arrive("w_right", from_right(gathered, 1, 2))
    add_modes(right, (2, 3), False)
    for part in range(2):
        far = af.at[across, pl.ds(2 * part * quarter, 2 * quarter)]
        arrive("w_across", (far, ag_r.at[1, 2 * grps + part]))
        add_modes(across, (2 * part, 2 * part + 1), part == 0)
    totals = []

    def first_picked():
        arrive("w_psc", (psc.at[pl.ds(0, grps - 1)], p_r.at[2]))
        picked = coarse_third(0)
        totals.append(picked)
        high, rest = halves(picked.T[:quarter])
        both = jnp.concatenate(
            [jnp.concatenate([high, high], axis=1), jnp.concatenate([rest, rest], axis=1)],
            axis=0,
        )
        terms = []
        for q in range(grps):
            term = dot_nn(both, psc[q])
            terms.append(term[:quarter] + term[quarter:])
        return terms

    final_sums = []

    def hand_back(part, mine):
        final_sums.append(coarse_part(part, mine))
        if part == PARTS - 1:
            coarse_first(1, sum(final_sums))
        for q in range(grps):
            ls[q, rows_of(part), :] = mine[:, q * LANES : (q + 1) * LANES]
        for step in (2, 1, 3):
            to = grp_at(step)
            remote(
                ls.at[to, rows_of(part)], lr.at[g, rows_of(part)], fin_s, fin_r, {"grp": to}
            ).start()

    exchange(1, acc[...], first_picked, hand_back)
    lr[g] = ls[g]

    def own_rows(blocks):
        lines = [
            jnp.concatenate(
                [block[mg * quarter : (mg + 1) * quarter] for mg in range(4)], axis=1
            )
            for block in blocks
        ]
        return jnp.concatenate(lines, axis=0)

    here = pl.ds(pl.multiple_of(g * LANES, LANES), LANES)
    lifted = dot_nn(own_rows([af[q, :, here] for q in range(grps)]), bd[g])
    acc[...] = st[...] - relax_weight * lifted
    coarse_second(1)
    arrive("w_fin", (lr.at[pl.ds(0, grps - 1)], fin_r))
    acc[...] -= relax_weight * dot_nn(own_rows([lr[q] for q in range(grps)]), bd[g])
    pk[g] = coarse_third(1) + totals[0]
    for step in (2, 1, 3):
        remote(pk.at[g], pk.at[g], k3_s, k3_r, {"grp": grp_at(step)}).start()
    basis = jnp.concatenate([ca[g], ca[g]], axis=0)
    arrive("w_k3", (pk.at[pl.ds(0, grps - 1)], k3_r))
    tall = jnp.concatenate([pk[q].T[:quarter] for q in range(grps)], axis=0)
    corr = dot_nn(jnp.concatenate(halves(tall), axis=1), basis)
    out[...] = acc[...] - coarse_weight * corr

    others = pl.ds(0, grps - 1)
    done = [
        (tb.at[others], ag_s.at[0]),
        (af.at[others], ag_s.at[1]),
        (ca.at[others], p_s.at[0]),
        (pa.at[others], p_s.at[1]),
        (psc.at[others], p_s.at[2]),
        (ls.at[others], fin_s),
        (pk.at[others], k3_s),
    ]
    for turn in range(ITERS):
        done += [
            (sb.at[turn, others], a2a_s.at[turn]),
            (zs.at[turn, pl.ds(0, LINKS - 1)], ex_s.at[turn]),
            (rs.at[turn, pl.ds(0, LINKS - 1)], ret_s.at[turn]),
            (pz.at[turn, pl.ds(0, zs_n - 1)], k1_s.at[turn]),
            (ks.at[turn, pl.ds(0, yc_n - 1)], k2_s.at[turn]),
        ]
    with jax.named_scope("w_sends"):
        for ref, sem in done:
            whole(ref, sem).wait_send()


def solution(mesh):
    subs, grps = mesh.shape["sub"], mesh.shape["grp"]
    zs_n = 8 if subs == 128 else 2
    yc_n = subs // zs_n
    sizes = (subs, grps, zs_n, yc_n)

    def body(
        schur,
        rhs,
        start,
        project,
        coarse_basis,
        owner_of_face,
        mortar_of_face,
        mortar_order,
        subdomain_map,
        vertex_ids,
    ):
        rows, cols = schur.shape[1], schur.shape[2]
        part = cols // grps
        wide = rhs.shape[2]
        faces = owner_of_face.shape[1]
        block = LANES
        dma = pltpu.SemaphoreType.DMA
        vmem = pltpu.VMEM
        scratch = [
            vmem((grps, rows, part), BF16),
            vmem((wide, rows), F32),
            vmem((wide, rows), F32),
            vmem((grps, wide, rows), BF16),
            vmem((grps, wide, rows), BF16),
            vmem((grps,) + project.shape[1:], BF16),
            vmem((grps,) + coarse_basis.shape[1:], BF16),
            vmem((grps, rows, rows), BF16),
            vmem((4, rows, rows), BF16),
            vmem((rows, LINKS * block), BF16),
            vmem((LINKS * block, 16 * MORT_OWN), BF16),
            vmem((8, 16 * MORT_OWN), F32),
            vmem((wide, rows), F32),
            vmem((wide, rows), F32),
            vmem((ITERS, grps, wide, block), BF16),
            vmem((ITERS, grps, wide, block), BF16),
            vmem((ITERS, LINKS, wide, block), BF16),
            vmem((ITERS, LINKS, wide, block), BF16),
            vmem((ITERS, LINKS, wide, block), BF16),
            vmem((ITERS, LINKS, wide, block), BF16),
            vmem((grps, wide, block), BF16),
            vmem((grps, wide, block), BF16),
            vmem((4, 2 * NCV, rows), BF16),
            vmem((grps, 2 * NCV, rows), BF16),
            vmem((yc_n * NCV, zs_n * NCV), BF16),
            vmem((ITERS, NCV, LANES), F32),
            vmem((ITERS, zs_n, NCV, LANES), F32),
            vmem((ITERS, yc_n, NCV, LANES), F32),
            vmem((ITERS, yc_n, NCV, LANES), F32),
            vmem((grps, NCV, LANES), F32),
            vmem((faces, subs), jnp.int32),
            vmem((faces, subs), jnp.int32),
            vmem((MORT_OWN, subs), jnp.int32),
            vmem((1, subs), jnp.int32),
            vmem((NCV, subs), jnp.int32),
            dma((9 + grps,)),
            dma((2,)),
            dma((2, 2 * grps + 2)),
            dma((ITERS,)),
            dma((ITERS, PARTS)),
            dma((ITERS,)),
            dma((ITERS, PARTS)),
            dma((ITERS,)),
            dma((ITERS, PARTS)),
            dma((3,)),
            dma((3,)),
            dma((ITERS,)),
            dma((ITERS,)),
            dma((ITERS,)),
            dma((ITERS,)),
            dma(()),
            dma(()),
            dma(()),
            dma(()),
        ]
        operands = (
            schur[0],
            rhs[0].T,
            start[0].T,
            project[0],
            coarse_basis[0],
            owner_of_face[:, :, 0].T,
            mortar_of_face.T,
            mortar_order.T,
            subdomain_map.reshape(1, subs),
            vertex_ids.T,
        )
        result = pl.pallas_call(
            functools.partial(kernel, sizes),
            out_shape=jax.ShapeDtypeStruct((wide, rows), F32),
            in_specs=[pl.BlockSpec(memory_space=pltpu.HBM)] * 10,
            out_specs=pl.BlockSpec(memory_space=pltpu.VMEM),
            scratch_shapes=scratch,
            compiler_params=pltpu.CompilerParams(
                collective_id=0, has_side_effects=True, vmem_limit_bytes=44 * 1024 * 1024
            ),
        )(*(pltpu.with_memory_space_constraint(value, pltpu.HBM) for value in operands))
        return result.T[None]

    split = P("sub", "grp", None)
    return jax.shard_map(
        body,
        mesh=mesh,
        in_specs=(split, split, split, split, P("sub", None, "grp"), P(), P(), P(), P(), P()),
        out_specs=split,
        check_vma=False,
    )
```

time: 82.6 us -> 75.4 us (0.913)
  Pallas kernels: 80 us -> 74.5 us
  local copies, waits for them, and re-layouts: 1.77 us -> 0.75 us
    pallas_call x1, Pallas kernels: 80 us -> 74.5 us  [body(): pl.pallas_call(functools.partial(kernel, sizes), out_shape=jax.ShapeDtype...]
    unnamed x1, local copies, waits for them, and re-layouts: 1.77 us -> 0.75 us
where the time goes in v2:
time: 75.4 us; the launch traced here: 75.3 us
  Pallas kernels  74.5 us (99%)
    pallas_call x1, Pallas kernels, body(): pl.pallas_call(functools.partial(kernel, sizes), out_shape=jax.ShapeDtype...  74.5 us

profile of v2, /device:TPU:1, one launch (start us, length us, event | category | flops | bytes accessed | tf_op | source)
XLA Modules:
  0.0 75.3 jit_solution(3103578700432196780)
XLA Ops:
  0.0 74.5 %shard_map.100 = f32[192,512]{1,0:T(8,128)S(1)} custom-call(bf16[512,2048]{1,0:T(8,128)(2,1)} %bitcast.20, f32[192,512]{1,0:T(8,128)} %bitcast.21, f32[192,512]{1,0:T(8,128)} %bitcast.22, bf16[8,4096]{1,0:T(8,128)(2,1)} %bitcast.23, bf16[8,512]{1,0:T(8,128)(2,1)} %bitcast.26, s32[32,128]{1,0:T(8,128)} %bitcast.24, s32[32,128]{1,0:T(8,128)} %bitcast.25, ...), custom_call_target="tpu_custom_call" | custom-call | tf_op jit(solution)/shard_map/pallas_call | solution.py:742
  74.5 0.7 copy.12

commit v3 on v2

--- a/solution.py
+++ b/solution.py
@@ -10,6 +10,7 @@
 MORT_OWN = 16
 REACH = 2
 LINKS = 2 * REACH + 1
+HALF_LINKS = REACH + 1
 CAP = 8
 NCV = 8
 ITERS = 2
@@ -77,6 +78,10 @@
     ls,
     lr,
     qm,
+    qs,
+    qr,
+    gm,
+    av,
     psc,
     dm,
     ps,
@@ -142,14 +147,6 @@
             for ref, sem in parts:
                 whole(ref, sem).wait_recv()
 
-    barrier = pltpu.get_barrier_semaphore()
-    partners = [{"sub": lax.rem(z + step, zs_n) * yc_n + yc} for step in range(1, zs_n)]
-    partners += [{"sub": z * yc_n + lax.rem(yc + step, yc_n)} for step in range(1, yc_n)]
-    partners += [{"sub": sub_at(step)} for step in (-2, -1, 1, 2)]
-    partners += [{"grp": grp_at(step)} for step in range(1, grps)]
-    for where in partners:
-        pl.semaphore_signal(barrier, inc=1, device_id=where, device_id_type=MESH)
-
     loads = [
         pltpu.make_async_copy(start, st, lsem.at[0]),
         pltpu.make_async_copy(owner_t, own_tab, lsem.at[1]),
@@ -167,7 +164,17 @@
                 schur.at[:, pl.ds(q * cols, cols)], s4.at[q], lsem.at[9 + q]
             )
         )
-    for load in loads:
+    loads[0].start()
+
+    barrier = pltpu.get_barrier_semaphore()
+    partners = [{"sub": lax.rem(z + step, zs_n) * yc_n + yc} for step in range(1, zs_n)]
+    partners += [{"sub": z * yc_n + lax.rem(yc + step, yc_n)} for step in range(1, yc_n)]
+    partners += [{"sub": sub_at(step)} for step in (-2, -1, 1, 2)]
+    partners += [{"grp": grp_at(step)} for step in range(1, grps)]
+    for where in partners:
+        pl.semaphore_signal(barrier, inc=1, device_id=where, device_id_type=MESH)
+
+    for load in loads[1:]:
         load.start()
 
     with jax.named_scope("w_start"):
@@ -217,7 +224,6 @@
     for i in range(0, grps, 2):
         gather_send(gathered, i)
 
-    ps[...] = jnp.zeros_like(ps)
     for load in loads[1:6]:
         load.wait()
     stacked = jnp.concatenate(
@@ -297,7 +303,7 @@
         fac[pl.ds(mg, 1), :] = jnp.where(keep, inverse, 0.0)
 
     vertex_b = vertex_all.astype(BF16)
-    d_rows, d_cols = dm.shape
+    d_rows, d_cols = dm.shape[0] // 2, dm.shape[1]
     here = jnp.where(
         iota((d_rows, subs), 1) == z * yc_n + jnp.right_shift(iota((d_rows, subs), 0), 3), 1.0, 0.0
     ).astype(BF16)
@@ -307,16 +313,26 @@
         axis=1,
         keepdims=True,
     )
-    there = jnp.where(
-        iota((subs, d_cols), 0) == jnp.right_shift(iota((subs, d_cols), 1), 3) * yc_n + yc, 1.0, 0.0
-    ).astype(BF16)
-    given = dot_nn(vertex_b, there)
-    given = jnp.sum(
-        jnp.where(iota((NCV, d_cols), 0) == (iota((NCV, d_cols), 1) & 7), given, 0.0),
-        axis=0,
-        keepdims=True,
-    )
-    dm[...] = jnp.where(wanted == given, 1.0, 0.0).astype(BF16)
+    block = zs_n * NCV
+    places = iota((subs, block), 0)
+    corner = iota((subs, block), 1)
+    met = []
+    for link in range(LINKS):
+        sender = jnp.right_shift(corner, 3) * yc_n + yc + (subs + REACH - link)
+        there = jnp.where(places == (sender & (subs - 1)), 1.0, 0.0).astype(BF16)
+        given = dot_nn(vertex_b, there)
+        given = jnp.sum(
+            jnp.where(iota((NCV, block), 0) == (iota((NCV, block), 1) & 7), given, 0.0),
+            axis=0,
+            keepdims=True,
+        )
+        met.append(jnp.where(wanted == given, 1.0, 0.0))
+    met.append(jnp.zeros_like(met[0]))
+    for i in range(HALF_LINKS):
+        for side in range(2):
+            dm[pl.ds(side * d_rows, d_rows), pl.ds(i * block, block)] = met[
+                side * HALF_LINKS + i
+            ].astype(BF16)
 
     lane = iota((CAP, LANES), 1)
     row8 = iota((CAP, 4 * LANES), 0)
@@ -334,7 +350,7 @@
             bd[q, pl.ds(pl.multiple_of(i * 16, 16), 16), :] = both
             return carry
 
-        lax.fori_loop(0, pa.shape[2] // LANES, step, 0, unroll=4)
+        lax.fori_loop(0, pa.shape[2] // LANES, step, 0, unroll=8)
 
     def fold_block(q, s_block):
         wide = dot_nt(s_block, bd[q]).astype(BF16)
@@ -343,12 +359,10 @@
                 :, mg * LANES : (mg + 1) * LANES
             ]
 
-    def fold_coarse(q):
-        both = jnp.concatenate(halves(dot_nt(ca[q], bd[q])), axis=0)
+    def fold_coarse():
+        both = jnp.concatenate(halves(dot_nt(ca[g], bd[g])), axis=0)
         for mg in range(4):
-            qm[mg, :, pl.ds(pl.multiple_of(q * LANES, LANES), LANES)] = both[
-                :, mg * LANES : (mg + 1) * LANES
-            ]
+            qm[g, pl.ds(mg * 2 * NCV, 2 * NCV), :] = both[:, mg * LANES : (mg + 1) * LANES]
 
     loads[6].wait()
     loads[7].wait()
@@ -359,6 +373,11 @@
             load.wait()
     for i in range(grps):
         gather_forward(gathered, 0, i)
+    fold_coarse()
+    for i, ref in enumerate((ca, qm)):
+        for step in (2, 1, 3):
+            where = {"grp": grp_at(step)}
+            remote(ref.at[g], ref.at[g], p_s.at[i], p_r.at[i], where).start()
 
     def add_block(q):
         acc[...] += dot_nt(tb[q], s4[q])
@@ -378,7 +397,16 @@
     def rows_of(part):
         return pl.ds(part * span, span)
 
-    def exchange(turn, residual, picked, deliver):
+    def swap_out(turn, part, q):
+        remote(
+            sb.at[turn, q, rows_of(part)],
+            ar.at[turn, g, rows_of(part)],
+            a2a_s.at[turn],
+            a2a_r.at[turn, part],
+            {"grp": q},
+        ).start()
+
+    def swap_all(residual):
         residual = residual.astype(BF16)
         for part in range(PARTS):
             first = part * groups
@@ -386,26 +414,44 @@
             coeffs = dot_nt(residual, modes).astype(BF16)
             for q in range(grps):
                 for mg in range(groups):
-                    sb[turn, q, pl.ds((first + mg) * quarter, quarter), :] = coeffs[
+                    sb[0, q, pl.ds((first + mg) * quarter, quarter), :] = coeffs[
                         q * quarter : (q + 1) * quarter, mg * LANES : (mg + 1) * LANES
                     ]
-            for i in (2, 1, 3):
-                to = grp_at(i)
-                remote(
-                    sb.at[turn, to, rows_of(part)],
-                    ar.at[turn, g, rows_of(part)],
-                    a2a_s.at[turn],
-                    a2a_r.at[turn, part],
-                    {"grp": to},
-                ).start()
-        ar[turn, g] = sb[turn, g]
+            for step in (2, 1, 3):
+                swap_out(0, part, grp_at(step))
+        ar[0, g] = sb[0, g]
+
+    def swap_quarter(q, own):
+        at = pl.ds(pl.multiple_of(q * quarter, quarter), quarter)
+        coeffs = dot_nt(acc[at, :].astype(BF16), bd[g]).astype(BF16)
+        tall = jnp.concatenate(
+            [coeffs[:, mg * LANES : (mg + 1) * LANES] for mg in range(4)], axis=0
+        )
+        if own:
+            ar[1, g] = tall
+            return
+        sb[1, q] = tall
+        for part in range(PARTS):
+            swap_out(1, part, q)
+
+    def exchange(turn, picked, deliver):
+        partials = []
         if turn == 0:
-            for i, ref in enumerate((ca, pa)):
-                for step in (2, 1, 3):
-                    where = {"grp": grp_at(step)}
-                    remote(ref.at[g], ref.at[g], p_s.at[i], p_r.at[i], where).start()
+            for step in (2, 1, 3):
+                where = {"grp": grp_at(step)}
+                remote(pa.at[g], pa.at[g], p_s.at[4], p_r.at[4], where).start()
+            others = pl.ds(0, grps - 1)
             fold_block(g, s4[g])
-            fold_coarse(g)
+            arrive("w_extra", (ca.at[others], p_r.at[0]), (qm.at[others], p_r.at[1]))
+            slots = dot_nn(
+                jnp.concatenate([qm[q] for q in range(grps)], axis=1), wm[...]
+            ).astype(BF16)
+            for link in (0, 4, 1, 3, 2):
+                piece = slots[:, link * LANES : (link + 1) * LANES]
+                if link == REACH:
+                    qr[link] = piece
+                    continue
+                qs[link] = piece
         terms = None if picked is None else picked()
         for part in range(PARTS):
             arrive("w_a2a", (ar.at[turn, pl.ds(0, grps - 1), rows_of(part)], a2a_r.at[turn, part]))
@@ -435,8 +481,10 @@
                     {"sub": sub_at(link - REACH)},
                 ).start()
         if turn == 0:
-            others = pl.ds(0, grps - 1)
-            arrive("w_extra", (ca.at[others], p_r.at[0]), (pa.at[others], p_r.at[1]))
+            for link in (0, 4, 1, 3):
+                where = {"sub": sub_at(link - REACH)}
+                remote(qs.at[link], qr.at[link], p_s.at[3], p_r.at[3], where).start()
+            arrive("w_p", (pa.at[others], p_r.at[4]))
             for i in range(grps - 1):
                 build_block(grp_at(i + 1))
         for part in range(PARTS):
@@ -467,11 +515,18 @@
                     ret_r.at[turn, part],
                     {"sub": sub_at(REACH - link)},
                 ).start()
+            if turn == 0:
+                av[rows_of(part), :] = averages
+            else:
+                partials.append(coarse_part(part, averages))
+        if turn == 1:
+            coarse_first(1, sum(partials[1:], partials[0]))
+            lift_first()
+            coarse_second(1)
         if turn == 0:
             for i in range(grps - 1):
                 q = grp_at(i + 1)
                 fold_block(q, s4[q])
-                fold_coarse(q)
             spread = dot_nt(ca[0], s4[0])
             for q in range(1, grps):
                 spread = spread + dot_nt(ca[q], s4[q])
@@ -482,6 +537,10 @@
             for step in (2, 1, 3):
                 where = {"grp": grp_at(step)}
                 remote(psc.at[g], psc.at[g], p_s.at[2], p_r.at[2], where).start()
+            arrive("w_q", (qr.at[pl.ds(0, LINKS - 1)], p_r.at[3]))
+            build_owner()
+            partials = [coarse_part(part, av[rows_of(part), :]) for part in range(PARTS)]
+            coarse_first(0, sum(partials[1:], partials[0]))
         for part in range(PARTS):
             arrive("w_ret", (rr.at[turn, pl.ds(0, LINKS - 1), rows_of(part)], ret_r.at[turn, part]))
             answered = jnp.concatenate(
@@ -489,16 +548,39 @@
             )
             deliver(part, dot_nt(answered, wm[...]).astype(BF16))
 
-    def coarse_part(part, mine):
-        value = dot_nt(qm[part * groups], mine[:quarter])
-        for mg in range(1, groups):
-            value = value + dot_nt(
-                qm[part * groups + mg], mine[mg * quarter : (mg + 1) * quarter]
+    def build_owner():
+        lines = []
+        for link in range(LINKS):
+            both = dot_nn(qr[link], vm[pl.ds(link * LANES, LANES), :])
+            lines.append(
+                [
+                    both[mg * 2 * NCV : mg * 2 * NCV + NCV]
+                    + both[mg * 2 * NCV + NCV : (mg + 1) * 2 * NCV]
+                    for mg in range(4)
+                ]
             )
-        return value[:NCV] + value[NCV:]
+        for mg in range(4):
+            full = jnp.concatenate([line[mg] for line in lines], axis=0)
+            gm[mg] = jnp.concatenate(halves(full), axis=0)
+
+    def coarse_part(part, averages):
+        gap = jnp.zeros((LANES // 2 - quarter, averages.shape[1]), BF16)
+        total = None
+        for mg in range(groups):
+            line = averages[mg * quarter : (mg + 1) * quarter]
+            twice = jnp.concatenate([line, gap, line, gap], axis=0)
+            value = dot_nt(gm[part * groups + mg], twice)
+            total = value if total is None else total + value
+        return total[: LINKS * NCV] + total[LINKS * NCV :]
+
+    side = iota((HALF_LINKS * NCV, LANES), 1) < LANES // 2
 
     def coarse_first(turn, value):
-        ps[turn, :, pl.ds(0, quarter)] = value
+        first = value[: HALF_LINKS * NCV]
+        second = jnp.concatenate(
+            [value[HALF_LINKS * NCV :], jnp.zeros((NCV, LANES), F32)], axis=0
+        )
+        ps[turn] = jnp.where(side, first, second).astype(BF16)
         for step in range(zs_n - 1):
             to = lax.rem(z + step + 1, zs_n) * yc_n + yc
             remote(
@@ -508,8 +590,18 @@
 
     def coarse_second(turn):
         arrive("w_k1", (pz.at[turn, pl.ds(0, zs_n - 1)], k1_r.at[turn]))
-        high, rest = halves(pz[turn].reshape(zs_n * NCV, LANES))
-        value = dot_nn(dm[...], high) + dot_nn(dm[...], rest)
+        near = pz[turn].astype(F32)
+        lines = jnp.concatenate(
+            [
+                near[:, i * NCV : (i + 1) * NCV, :].reshape(zs_n * NCV, LANES)
+                for i in range(HALF_LINKS)
+            ],
+            axis=0,
+        ).astype(BF16)
+        value = dot_nn(dm[...], lines)
+        half_rows = value.shape[0] // 2
+        lane_of = iota((half_rows, LANES), 1)
+        value = jnp.where(lane_of < LANES // 2, value[:half_rows], value[half_rows:])
         ks[turn] = value.reshape(yc_n, NCV, LANES)
         for step in range(yc_n - 1):
             to = lax.rem(yc + step + 1, yc_n)
@@ -524,20 +616,17 @@
 
     def coarse_third(turn):
         arrive("w_k2", (kr.at[turn, pl.ds(0, yc_n - 1)], k2_r.at[turn]))
-        return jnp.sum(kr[turn], axis=0)
+        total = jnp.sum(kr[turn], axis=0)
+        return total + pltpu.roll(total, LANES // 2, 1)
 
     gathered = gather_plan(af, 1)
-    sums = []
-
     def spread_out(part, mine):
         af[g, rows_of(part), :] = mine
         for i in range(part * groups, (part + 1) * groups, 2):
             gather_send(gathered, i)
-        sums.append(coarse_part(part, mine))
-        if part == PARTS - 1:
-            coarse_first(0, sum(sums))
-
-    exchange(0, prod[...], None, spread_out)
+
+    swap_all(prod[...])
+    exchange(0, None, spread_out)
 
     def add_modes(q, groups_of, fresh):
         at = pl.ds(pl.multiple_of(q * quarter, quarter), quarter)
@@ -548,23 +637,27 @@
         acc[at, :] = base[at, :] - relax_weight * value
 
     add_modes(g, (0, 1, 2, 3), True)
+    swap_quarter(g, True)
     gather_forward(gathered, 1, 0)
     gather_forward(gathered, 1, 1)
     arrive("w_left", from_left(gathered, 1, 1))
     add_modes(left, (0, 1), True)
     arrive("w_right", from_right(gathered, 1, 0))
     add_modes(right, (0, 1), True)
+    coarse_second(0)
     gather_forward(gathered, 1, 2)
     gather_forward(gathered, 1, 3)
-    coarse_second(0)
     arrive("w_left", from_left(gathered, 1, 3))
     add_modes(left, (2, 3), False)
+    swap_quarter(left, False)
     arrive("w_right", from_right(gathered, 1, 2))
     add_modes(right, (2, 3), False)
+    swap_quarter(right, False)
     for part in range(2):
         far = af.at[across, pl.ds(2 * part * quarter, 2 * quarter)]
         arrive("w_across", (far, ag_r.at[1, 2 * grps + part]))
         add_modes(across, (2 * part, 2 * part + 1), part == 0)
+    swap_quarter(across, False)
     totals = []
 
     def first_picked():
@@ -582,12 +675,7 @@
             terms.append(term[:quarter] + term[quarter:])
         return terms
 
-    final_sums = []
-
     def hand_back(part, mine):
-        final_sums.append(coarse_part(part, mine))
-        if part == PARTS - 1:
-            coarse_first(1, sum(final_sums))
         for q in range(grps):
             ls[q, rows_of(part), :] = mine[:, q * LANES : (q + 1) * LANES]
         for step in (2, 1, 3):
@@ -595,9 +683,6 @@
             remote(
                 ls.at[to, rows_of(part)], lr.at[g, rows_of(part)], fin_s, fin_r, {"grp": to}
             ).start()
-
-    exchange(1, acc[...], first_picked, hand_back)
-    lr[g] = ls[g]
 
     def own_rows(blocks):
         lines = [
@@ -608,15 +693,18 @@
         ]
         return jnp.concatenate(lines, axis=0)
 
-    here = pl.ds(pl.multiple_of(g * LANES, LANES), LANES)
-    lifted = dot_nn(own_rows([af[q, :, here] for q in range(grps)]), bd[g])
-    acc[...] = st[...] - relax_weight * lifted
-    coarse_second(1)
-    arrive("w_fin", (lr.at[pl.ds(0, grps - 1)], fin_r))
-    acc[...] -= relax_weight * dot_nn(own_rows([lr[q] for q in range(grps)]), bd[g])
+    def lift_first():
+        here = pl.ds(pl.multiple_of(g * LANES, LANES), LANES)
+        lifted = dot_nn(own_rows([af[q, :, here] for q in range(grps)]), bd[g])
+        acc[...] = st[...] - relax_weight * lifted
+
+    exchange(1, first_picked, hand_back)
+    lr[g] = ls[g]
     pk[g] = coarse_third(1) + totals[0]
     for step in (2, 1, 3):
         remote(pk.at[g], pk.at[g], k3_s, k3_r, {"grp": grp_at(step)}).start()
+    arrive("w_fin", (lr.at[pl.ds(0, grps - 1)], fin_r))
+    acc[...] -= relax_weight * dot_nn(own_rows([lr[q] for q in range(grps)]), bd[g])
     basis = jnp.concatenate([ca[g], ca[g]], axis=0)
     arrive("w_k3", (pk.at[pl.ds(0, grps - 1)], k3_r))
     tall = jnp.concatenate([pk[q].T[:quarter] for q in range(grps)], axis=0)
@@ -628,8 +716,10 @@
         (tb.at[others], ag_s.at[0]),
         (af.at[others], ag_s.at[1]),
         (ca.at[others], p_s.at[0]),
-        (pa.at[others], p_s.at[1]),
+        (qm.at[others], p_s.at[1]),
+        (pa.at[others], p_s.at[4]),
         (psc.at[others], p_s.at[2]),
+        (qs.at[pl.ds(0, LINKS - 1)], p_s.at[3]),
         (ls.at[others], fin_s),
         (pk.at[others], k3_s),
     ]
@@ -694,11 +784,15 @@
             vmem((ITERS, LINKS, wide, block), BF16),
             vmem((grps, wide, block), BF16),
             vmem((grps, wide, block), BF16),
-            vmem((4, 2 * NCV, rows), BF16),
+            vmem((grps, 8 * NCV, block), BF16),
+            vmem((LINKS, 8 * NCV, block), BF16),
+            vmem((LINKS, 8 * NCV, block), BF16),
+            vmem((4, 2 * LINKS * NCV, 16 * MORT_OWN), BF16),
+            vmem((wide, 16 * MORT_OWN), BF16),
             vmem((grps, 2 * NCV, rows), BF16),
-            vmem((yc_n * NCV, zs_n * NCV), BF16),
-            vmem((ITERS, NCV, LANES), F32),
-            vmem((ITERS, zs_n, NCV, LANES), F32),
+            vmem((2 * yc_n * NCV, HALF_LINKS * zs_n * NCV), BF16),
+            vmem((ITERS, HALF_LINKS * NCV, LANES), BF16),
+            vmem((ITERS, zs_n, HALF_LINKS * NCV, LANES), BF16),
             vmem((ITERS, yc_n, NCV, LANES), F32),
             vmem((ITERS, yc_n, NCV, LANES), F32),
             vmem((grps, NCV, LANES), F32),
@@ -716,8 +810,8 @@
             dma((ITERS, PARTS)),
             dma((ITERS,)),
             dma((ITERS, PARTS)),
-            dma((3,)),
-            dma((3,)),
+            dma((5,)),
+            dma((5,)),
             dma((ITERS,)),
             dma((ITERS,)),
             dma((ITERS,)),

time: 75.4 us -> 71.2 us (0.944)
  Pallas kernels: 74.5 us -> 70.3 us
    pallas_call x1, Pallas kernels: 74.5 us -> 70.3 us  [body(): pl.pallas_call(functools.partial(kernel, sizes), out_shape=jax.ShapeDtype...]
where the time goes in v3:
time: 71.2 us; the launch traced here: 71.1 us
  Pallas kernels  70.3 us (99%)
  local copies, waits for them, and re-layouts  0.75 us (1%)
    pallas_call x1, Pallas kernels, body(): pl.pallas_call(functools.partial(kernel, sizes), out_shape=jax.ShapeDtype...  70.3 us

profile of v3, /device:TPU:1, one launch (start us, length us, event | category | flops | bytes accessed | tf_op | source)
XLA Modules:
  0.0 71.1 jit_solution(7111090439489120357)
XLA Ops:
  0.0 70.3 %shard_map.100 = f32[192,512]{1,0:T(8,128)S(1)} custom-call(bf16[512,2048]{1,0:T(8,128)(2,1)} %bitcast.20, f32[192,512]{1,0:T(8,128)} %bitcast.21, f32[192,512]{1,0:T(8,128)} %bitcast.22, bf16[8,4096]{1,0:T(8,128)(2,1)} %bitcast.23, bf16[8,512]{1,0:T(8,128)(2,1)} %bitcast.26, s32[32,128]{1,0:T(8,128)} %bitcast.24, s32[32,128]{1,0:T(8,128)} %bitcast.25, ...), custom_call_target="tpu_custom_call" | custom-call | tf_op jit(solution)/shard_map/pallas_call | solution.py:836
  70.3 0.7 %copy.12 = f32[1,512,192]{1,2,0:T(8,128)} copy(f32[1,512,192]{1,2,0:T(8,128)S(1)} %bitcast.19) | data formatting | bytes 786432

commit v4 on v3

--- a/solution.py
+++ b/solution.py
@@ -113,6 +113,7 @@
     k3_r,
     fin_s,
     fin_r,
+    news,
 ):
     subs, grps, zs_n, yc_n = sizes
     s = lax.axis_index("sub")
@@ -167,8 +168,13 @@
     loads[0].start()
 
     barrier = pltpu.get_barrier_semaphore()
-    partners = [{"sub": lax.rem(z + step, zs_n) * yc_n + yc} for step in range(1, zs_n)]
-    partners += [{"sub": z * yc_n + lax.rem(yc + step, yc_n)} for step in range(1, yc_n)]
+    line = [{"sub": lax.rem(z + step, zs_n) * yc_n + yc} for step in (1, zs_n - 1)]
+    plane = [
+        {"sub": z * yc_n + lax.rem(yc + step, yc_n)} for step in (2, yc_n - 2)
+    ]
+    cross = yc - lax.rem(yc, 2) + 1 - lax.rem(yc, 2)
+    mates = [{"sub": z * yc_n + lax.rem(cross + step, yc_n)} for step in (0, 2, yc_n - 2)]
+    partners = line + plane + mates
     partners += [{"sub": sub_at(step)} for step in (-2, -1, 1, 2)]
     partners += [{"grp": grp_at(step)} for step in range(1, grps)]
     for where in partners:
@@ -202,8 +208,12 @@
         _, send, _ = plan
         send(g, i, i, to_right)
         send(g, i + 1, grps + i + 1, to_left)
-        send(g, i + 1, i + 1, to_right)
-        send(g, i, grps + i, to_left)
+
+    def gather_rest(plan):
+        _, send, _ = plan
+        for i in range(0, grps, 2):
+            send(g, i + 1, i + 1, to_right)
+            send(g, i, grps + i, to_left)
 
     def from_left(plan, turn, i):
         return plan[0](left, i), ag_r.at[turn, i]
@@ -223,6 +233,21 @@
     gathered = gather_plan(tb, 0)
     for i in range(0, grps, 2):
         gather_send(gathered, i)
+    gather_rest(gathered)
+
+    def spread_news(step):
+        for i, pair in enumerate((line, plane)):
+            for where in pair:
+                pl.semaphore_signal(
+                    news.at[i, step], inc=1, device_id=where, device_id_type=MESH
+                )
+
+    def take_news(step):
+        with jax.named_scope("w_news"):
+            for i in range(2):
+                pl.semaphore_wait(news.at[i, step], 2)
+
+    spread_news(0)
 
     for load in loads[1:6]:
         load.wait()
@@ -368,11 +393,17 @@
     loads[7].wait()
     with jax.named_scope("c_block"):
         build_block(g)
+    take_news(0)
+    spread_news(1)
     with jax.named_scope("w_loads"):
         for load in loads[8:]:
             load.wait()
     for i in range(grps):
         gather_forward(gathered, 0, i)
+        if i == 1:
+            take_news(1)
+            spread_news(2)
+    take_news(2)
     fold_coarse()
     for i, ref in enumerate((ca, qm)):
         for step in (2, 1, 3):
@@ -524,6 +555,10 @@
             lift_first()
             coarse_second(1)
         if turn == 0:
+            arrive("w_q", (qr.at[pl.ds(0, LINKS - 1)], p_r.at[3]))
+            build_owner()
+            partials = [coarse_part(part, av[rows_of(part), :]) for part in range(PARTS)]
+            coarse_first(0, sum(partials[1:], partials[0]))
             for i in range(grps - 1):
                 q = grp_at(i + 1)
                 fold_block(q, s4[q])
@@ -537,10 +572,6 @@
             for step in (2, 1, 3):
                 where = {"grp": grp_at(step)}
                 remote(psc.at[g], psc.at[g], p_s.at[2], p_r.at[2], where).start()
-            arrive("w_q", (qr.at[pl.ds(0, LINKS - 1)], p_r.at[3]))
-            build_owner()
-            partials = [coarse_part(part, av[rows_of(part), :]) for part in range(PARTS)]
-            coarse_first(0, sum(partials[1:], partials[0]))
         for part in range(PARTS):
             arrive("w_ret", (rr.at[turn, pl.ds(0, LINKS - 1), rows_of(part)], ret_r.at[turn, part]))
             answered = jnp.concatenate(
@@ -624,6 +655,8 @@
         af[g, rows_of(part), :] = mine
         for i in range(part * groups, (part + 1) * groups, 2):
             gather_send(gathered, i)
+        if part == PARTS - 1:
+            gather_rest(gathered)
 
     swap_all(prod[...])
     exchange(0, None, spread_out)
@@ -638,15 +671,13 @@
 
     add_modes(g, (0, 1, 2, 3), True)
     swap_quarter(g, True)
-    gather_forward(gathered, 1, 0)
-    gather_forward(gathered, 1, 1)
+    for i in range(grps):
+        gather_forward(gathered, 1, i)
+    coarse_second(0)
     arrive("w_left", from_left(gathered, 1, 1))
     add_modes(left, (0, 1), True)
     arrive("w_right", from_right(gathered, 1, 0))
     add_modes(right, (0, 1), True)
-    coarse_second(0)
-    gather_forward(gathered, 1, 2)
-    gather_forward(gathered, 1, 3)
     arrive("w_left", from_left(gathered, 1, 3))
     add_modes(left, (2, 3), False)
     swap_quarter(left, False)
@@ -820,6 +851,7 @@
             dma(()),
             dma(()),
             dma(()),
+            pltpu.SemaphoreType.REGULAR((2, 3)),
         ]
         operands = (
             schur[0],

time: 71.2 us -> 68.7 us (0.965)
  Pallas kernels: 70.3 us -> 67.8 us
    pallas_call x1, Pallas kernels: 70.3 us -> 67.8 us  [body(): pl.pallas_call(functools.partial(kernel, sizes), out_shape=jax.ShapeDtype...]
where the time goes in v4:
time: 68.7 us; the launch traced here: 68.6 us
  Pallas kernels  67.8 us (99%)
  local copies, waits for them, and re-layouts  0.75 us (1%)
    pallas_call x1, Pallas kernels, body(): pl.pallas_call(functools.partial(kernel, sizes), out_shape=jax.ShapeDtype...  67.8 us

profile of v4, /device:TPU:1, one launch (start us, length us, event | category | flops | bytes accessed | tf_op | source)
XLA Modules:
  0.0 68.6 jit_solution(11546137939203310669)
XLA Ops:
  0.0 67.8 %shard_map.100 = f32[192,512]{1,0:T(8,128)S(1)} custom-call(bf16[512,2048]{1,0:T(8,128)(2,1)} %bitcast.20, f32[192,512]{1,0:T(8,128)} %bitcast.21, f32[192,512]{1,0:T(8,128)} %bitcast.22, bf16[8,4096]{1,0:T(8,128)(2,1)} %bitcast.23, bf16[8,512]{1,0:T(8,128)(2,1)} %bitcast.26, s32[32,128]{1,0:T(8,128)} %bitcast.24, s32[32,128]{1,0:T(8,128)} %bitcast.25, ...), custom_call_target="tpu_custom_call" | custom-call | tf_op jit(solution)/shard_map/pallas_call | solution.py:868
  67.8 0.7 %copy.12 = f32[1,512,192]{1,2,0:T(8,128)} copy(f32[1,512,192]{1,2,0:T(8,128)S(1)} %bitcast.19) | data formatting | bytes 786432
